TPU v7x, 256 devices: a whole 4x4x8 slice. The times are simulated.
256 devices in a mesh: grp: 8 (over y, x_lo), seq: 32 (over x_hi, z, core).
Axes of the slice: x: 4 (x_hi: 2, x_lo: 2; x = x_hi * 2 + x_lo), y: 4, z: 8, core: 2. Of those that a mesh axis runs over, the one named last changes fastest.
Arguments:
- queries: bfloat16 [16, 1024, 8192], P('grp', 'seq'), parts along dimension 0, may hold values from -400 to 400
- stretch_keys: bfloat16 [16, 1024, 1024], P('grp', 'seq'), parts along dimension 0, may hold values from -6 to 6
- stretch_values: bfloat16 [16, 1024, 1024], P('grp', 'seq'), parts along dimension 0, may hold values from -6 to 6
- cache_keys: bfloat16 [16, 2048, 1024], P('grp', 'seq'), parts along dimension 0, may hold values from -6 to 6
- cache_values: bfloat16 [16, 2048, 1024], P('grp', 'seq'), parts along dimension 0, may hold values from -6 to 6
- prefix_len: int32 [16], P('grp'), parts along dimension 0, may hold values from 16 to 2048, as said below
Outputs:
- attention: bfloat16 [16, 1024, 8192], P('grp', 'seq'), parts along dimension 0
- prefix_bounds: bfloat16 [16, 128, 2048], P('grp', 'seq'), parts along dimension 0
- stretch_bounds: bfloat16 [16, 64, 2048], P('grp', 'seq'), parts along dimension 0
There are 8 independent parts, one for each index of `grp`. A program takes and returns all parts, laid end to end along the dimension named above; each array names one. Nothing has to cross between parts.
Inputs may be any that keep to these rules, and one draw needn't show every extreme that they name: `prefix_len`: multiples of 16; some sequence of every group has 2048.
All inputs are finite; a program needn't handle non-finite values.
Results may differ from a plain program's by a relative error of at most 0.006.
Values may be sent and summed in bfloat16 or wider, within the bound.
No kernel may reach another device: no remote copies, remote signals or barrier semaphores. Data moves between devices by JAX's collectives and lax.ppermute only.
A program may use at most 128 MiB of HBM per device.

v0:
```python
import math

import jax
import jax.numpy as jnp
from jax import lax
from jax.experimental import pallas as pl
from jax.experimental.pallas import tpu as pltpu
from jax.sharding import PartitionSpec as P

HQ = 64
HK = 8
DH = 128
PAGE = 16
GROUP = HQ // HK
NEG = -1e30
QUAD = 4
RING = 8
KH = HK // QUAD
PHASES = ((0, 7, 1, 6, 2), (5, 3, 4))
SCALE = math.log2(math.e) / math.sqrt(DH)


def ring_perm(step):
    return [(i, (i // 16) * 16 + ((i // 2 + step) % RING) * 2 + i % 2) for i in range(32)]


def quad_perm(r):
    return [(i, i ^ ((r >> 1) * 16) ^ (r & 1)) for i in range(32)]


def corner(place_ref):
    return (place_ref[0] // 16) * 2 + place_ref[0] % 2


def pack_kv(s, place, cache_keys, cache_values, stretch_keys, stretch_values):
    pre, new = cache_keys.shape[1], stretch_keys.shape[1]

    def body(place_ref, ck, cv, sk, sv, *outs):
        own = corner(place_ref)
        for r in range(QUAD):
            for h in range(KH):
                at = pl.ds(pl.multiple_of((own ^ r) * (KH * DH) + h * DH, DH), DH)
                for kv, (old, fresh) in enumerate(((ck, sk), (cv, sv))):
                    outs[r][kv, h, :pre, :] = old[0, :, at]
                    outs[r][kv, h, pre:, :] = fresh[0, :, at]

    shape = (2, KH, pre + new, DH)
    spec = lambda x: pl.BlockSpec((1,) + x.shape[1:], lambda i: (s, 0, 0))
    arrays = (cache_keys, cache_values, stretch_keys, stretch_values)
    return pl.pallas_call(
        body,
        grid=(1,),
        in_specs=[pl.BlockSpec(memory_space=pltpu.SMEM)] + [spec(x) for x in arrays],
        out_specs=[pl.BlockSpec(shape, lambda i: (0, 0, 0, 0))] * QUAD,
        out_shape=[jax.ShapeDtypeStruct(shape, jnp.bfloat16)] * QUAD,
        name="pack_kv",
    )(place, *arrays)


def pack_q(place, queries):
    seqs, rows, _ = queries.shape

    def body(place_ref, q, *outs):
        own = corner(place_ref)
        for r in range(QUAD):
            for h in range(KH):
                for g in range(GROUP):
                    at = (own ^ r) * (KH * GROUP * DH) + (h * GROUP + g) * DH
                    outs[r][0, h, g * rows : (g + 1) * rows, :] = q[0, :, pl.ds(pl.multiple_of(at, DH), DH)]

    block = (1, KH, GROUP * rows, DH)
    return pl.pallas_call(
        body,
        grid=(seqs,),
        in_specs=[pl.BlockSpec(memory_space=pltpu.SMEM), pl.BlockSpec((1, rows, HQ * DH), lambda s: (s, 0, 0))],
        out_specs=[pl.BlockSpec(block, lambda s: (s, 0, 0, 0))] * QUAD,
        out_shape=[jax.ShapeDtypeStruct((seqs,) + block[1:], jnp.bfloat16)] * QUAD,
        name="pack_q",
    )(place, queries)


def unpack_out(place, pieces, rows):
    seqs = len(pieces)

    def body(place_ref, *refs):
        own = corner(place_ref)
        out = refs[-1]
        for s in range(seqs):
            for r in range(QUAD):
                for h in range(KH):
                    for g in range(GROUP):
                        at = (own ^ r) * (KH * GROUP * DH) + (h * GROUP + g) * DH
                        piece = refs[s * QUAD + r][h, g * rows : (g + 1) * rows, :]
                        out[s, :, pl.ds(pl.multiple_of(at, DH), DH)] = piece

    return pl.pallas_call(
        body,
        in_specs=[pl.BlockSpec(memory_space=pltpu.SMEM)] + [pl.BlockSpec(memory_space=pltpu.VMEM)] * (seqs * QUAD),
        out_specs=pl.BlockSpec(memory_space=pltpu.VMEM),
        out_shape=jax.ShapeDtypeStruct((seqs, rows, HQ * DH), jnp.bfloat16),
        name="unpack_out",
    )(place, *[p for one in pieces for p in one])


def bounds(place, prefix_len, cache_keys, stretch_keys):
    seqs, pre, width = cache_keys.shape
    new = stretch_keys.shape[1]

    def body(place_ref, len_ref, ck, sk, pre_out, new_out):
        first = place_ref[0] * (pre // PAGE)
        for s in range(seqs):
            for p in range(pre // PAGE):
                rows = ck[s, p * PAGE : (p + 1) * PAGE, :].astype(jnp.float32)
                live = (first + p) * PAGE < len_ref[s]
                low = jnp.where(live, jnp.min(rows, axis=0, keepdims=True), 0.0)
                high = jnp.where(live, jnp.max(rows, axis=0, keepdims=True), 0.0)
                pre_out[s, p : p + 1, :width] = low.astype(jnp.bfloat16)
                pre_out[s, p : p + 1, width:] = high.astype(jnp.bfloat16)
            for p in range(new // PAGE):
                rows = sk[s, p * PAGE : (p + 1) * PAGE, :].astype(jnp.float32)
                new_out[s, p : p + 1, :width] = jnp.min(rows, axis=0, keepdims=True).astype(jnp.bfloat16)
                new_out[s, p : p + 1, width:] = jnp.max(rows, axis=0, keepdims=True).astype(jnp.bfloat16)

    return pl.pallas_call(
        body,
        in_specs=[pl.BlockSpec(memory_space=pltpu.SMEM)] * 2 + [pl.BlockSpec(memory_space=pltpu.VMEM)] * 2,
        out_specs=[pl.BlockSpec(memory_space=pltpu.VMEM)] * 2,
        out_shape=[
            jax.ShapeDtypeStruct((seqs, pre // PAGE, 2 * width), jnp.bfloat16),
            jax.ShapeDtypeStruct((seqs, new // PAGE, 2 * width), jnp.bfloat16),
        ],
        name="page_bounds",
    )(place, prefix_len, cache_keys, stretch_keys)


def attend(s, place, prefix_len, queries, blocks, which, state, last, rows):
    count = len(blocks)
    tile = GROUP * rows
    pre = blocks[0][0].shape[3] - rows
    old_chunks = QUAD * pre // DH
    chunks = old_chunks + QUAD * rows // DH

    def body(*refs):
        place_ref, len_ref = refs[:2]
        q_refs = refs[2 : 2 + QUAD]
        k_refs = refs[2 + QUAD : 2 + QUAD + count]
        v_refs = refs[2 + QUAD + count : 2 + QUAD + 2 * count]
        rest = refs[2 + QUAD + 2 * count : -1]
        score_ref = refs[-1]
        if state is not None:
            mixed_in, top_in = rest[:2]
            rest = rest[2:]
        own = corner(place_ref)
        z = (place_ref[0] // 2) % RING
        lane = lax.broadcasted_iota(jnp.int32, (1, DH), 1)

        def shard(slot, d):
            peer = own ^ slot
            return (peer // 2) * 16 + peer % 2 + ((z + d) % RING) * 2

        def spread(first, width, d):
            pos = shard(first, d) * width + lane
            for k in range(1, DH // width):
                pos = jnp.where(lane >= k * width, shard(first + k, d) * width + lane - k * width, pos)
            return pos

        per = DH // pre
        fade = [
            [jnp.where(spread(c * per, pre, d) < len_ref[s], 0.0, NEG) for c in range(old_chunks)] for d in which
        ]
        new_pos = [spread(0, rows, d) for d in which]
        ones = jnp.ones((QUAD * (pre + rows), DH), jnp.bfloat16)

        def side(ref):
            old = ref[0, :, 0, :pre, :].reshape(QUAD * pre, DH)
            return jnp.concatenate([old, ref[0, :, 0, pre:, :].reshape(QUAD * rows, DH)], axis=0)

        def score(r):
            q = q_refs[r][0, 0]
            row_pos = shard(r, 0) * rows + lax.broadcasted_iota(jnp.int32, (tile, DH), 0) % rows
            top = None
            for b in range(count):
                part = lax.dot_general(
                    q, side(k_refs[b]), (((1,), (1,)), ((), ())), preferred_element_type=jnp.float32
                )
                for c in range(chunks):
                    piece = part[:, c * DH : (c + 1) * DH]
                    if c < old_chunks:
                        piece = piece + fade[b][c]
                    else:
                        piece = jnp.where(new_pos[b] <= row_pos, piece, NEG)
                    score_ref[r % 2, b * chunks + c] = piece
                    top = piece if top is None else jnp.maximum(top, piece)
            return top

        def mix(r, top):
            at = slice(r * tile, (r + 1) * tile)
            top = jnp.broadcast_to(jnp.max(top, axis=-1, keepdims=True), (tile, DH))
            if state is not None:
                old_top = top_in[0, at, :]
                top = jnp.maximum(top, old_top)
            mixed = None
            for b in range(count):
                weights = [
                    jnp.exp2((score_ref[r % 2, b * chunks + c] - top) * SCALE).astype(jnp.bfloat16)
                    for c in range(chunks)
                ]
                part = jnp.dot(
                    jnp.concatenate(weights, axis=1),
                    jnp.concatenate([side(v_refs[b]), ones], axis=1),
                    preferred_element_type=jnp.float32,
                )
                mixed = part if mixed is None else mixed + part
            total, mixed = mixed[:, DH:], mixed[:, :DH]
            if state is not None:
                shrink = jnp.exp2((old_top - top) * SCALE)
                mixed = mixed + mixed_in[0, at, :DH] * shrink
                total = total + mixed_in[0, at, DH:] * shrink
            if last:
                rest[r][0] = (mixed / total).astype(jnp.bfloat16)
            else:
                rest[0][0, at, :DH] = mixed
                rest[0][0, at, DH:] = total
                rest[1][0, at, :] = top

        tops = score(0)
        for r in range(QUAD):
            following = score(r + 1) if r + 1 < QUAD else None
            mix(r, tops)
            tops = following

    kv_shape = (1, QUAD, 1) + blocks[0][0].shape[3:]
    kv_spec = lambda x, i: pl.BlockSpec(kv_shape, lambda h: (min(i, x.shape[0] - 1), 0, h, 0, 0))
    state_specs = [
        pl.BlockSpec((1, QUAD * tile, 2 * DH), lambda h: (h, 0, 0)),
        pl.BlockSpec((1, QUAD * tile, DH), lambda h: (h, 0, 0)),
    ]
    in_specs = [pl.BlockSpec(memory_space=pltpu.SMEM)] * 2
    in_specs += [pl.BlockSpec((1, 1, tile, DH), lambda h: (s, h, 0, 0))] * QUAD
    in_specs += [kv_spec(k, 0) for k, _ in blocks] + [kv_spec(v, 1) for _, v in blocks]
    operands = [place, prefix_len, *queries, *[k for k, _ in blocks], *[v for _, v in blocks]]
    if state is not None:
        in_specs += state_specs
        operands += list(state)
    if last:
        out_specs = [pl.BlockSpec((1, tile, DH), lambda h: (h, 0, 0))] * QUAD
        out_shape = [jax.ShapeDtypeStruct((KH, tile, DH), jnp.bfloat16)] * QUAD
    else:
        out_specs = state_specs
        out_shape = [jax.ShapeDtypeStruct((KH, QUAD * tile, w), jnp.float32) for w in (2 * DH, DH)]
    pairs = KH * QUAD * tile * chunks * DH * count
    return pl.pallas_call(
        body,
        grid=(KH,),
        in_specs=in_specs,
        out_specs=out_specs,
        out_shape=out_shape,
        scratch_shapes=[pltpu.VMEM((2, count * chunks, tile, DH), jnp.float32)],
        cost_estimate=pl.CostEstimate(flops=4 * DH * pairs, transcendentals=pairs, bytes_accessed=4 << 20),
        name="attend",
    )(*operands)


def send(array, perm):
    return lax.ppermute(array, "seq", perm)


def run(queries, stretch_keys, stretch_values, cache_keys, cache_values, prefix_len):
    seqs, rows, _ = queries.shape
    place = lax.axis_index("seq").astype(jnp.int32).reshape(1)

    mine = []
    for s in range(seqs):
        pieces = pack_kv(s, place, cache_keys, cache_values, stretch_keys, stretch_values)
        got = [pieces[0]] + [send(pieces[r], quad_perm(r)) for r in range(1, QUAD)]
        mine.append(jnp.stack(got, axis=1))
    packed = pack_q(place, queries)
    q_tiles = [packed[0]] + [send(packed[r], quad_perm(r)) for r in range(1, QUAD)]
    prefix_bounds, stretch_bounds = bounds(place, prefix_len, cache_keys, stretch_keys)

    blocks = [{0: (m, m)} for m in mine]
    half = RING // 2
    for step in range(1, half):
        for s in range(seqs):
            forth = send(blocks[s][(1 - step) % RING][0], ring_perm(1))
            back = send(blocks[s][step - 1][0], ring_perm(-1))
            blocks[s][-step % RING] = (forth, forth)
            blocks[s][step] = (back, back)
    for s in range(seqs):
        forth = send(blocks[s][half + 1][0][:1], ring_perm(1))
        back = send(blocks[s][half - 1][1][1:], ring_perm(-1))
        blocks[s][half] = (forth, back)

    sent = []
    for s in range(seqs):
        state = None
        for n, which in enumerate(PHASES):
            last = n + 1 == len(PHASES)
            state = attend(
                s, place, prefix_len, q_tiles, [blocks[s][d] for d in which], which, state, last, rows
            )
        sent.append([state[0]] + [send(state[r], quad_perm(r)) for r in range(1, QUAD)])
    attention = unpack_out(place, sent, rows)
    return attention, prefix_bounds, stretch_bounds


def solution(mesh):
    return jax.shard_map(
        run,
        mesh=mesh,
        in_specs=(
            P("grp", "seq", None),
            P("grp", "seq", None),
            P("grp", "seq", None),
            P("grp", "seq", None),
            P("grp", "seq", None),
            P("grp"),
        ),
        out_specs=(P("grp", "seq", None), P("grp", "seq", None), P("grp", "seq", None)),
        check_vma=False,
    )
```

profile of v0, /device:TPU:7, one launch (start us, length us, event | category | flops | bytes accessed | tf_op | source)
XLA Modules:
  0.0 129.9 jit_solution(11063189940538109518)
XLA Ops:
  0.6 1.8 %pack_kv.3 = (bf16[2,2,96,128]{3,2,1,0:T(8,128)(2,1)}, bf16[2,2,96,128]{3,2,1,0:T(8,128)(2,1)}, bf16[2,2,96,128]{3,2,1,0:T(8,128)(2,1)}, bf16[2,2,96,128]{3,2,1,0:T(8,128)(2,1)}) custom-call(s32[1]{0:T(128)} %bitcast.place_ref.refs_0_, bf16[2,64,1024]{2,1,0:T(8,128)(2,1)} %ck.5, bf16[2,64,1024]{2,1,0:T(8,128)(2,1)} %cv.3, bf16[2,32,1024]{2,1,0:T(8,128)(2,1)} %sk.5, ...), custom_call_target="tpu_custom_call" | custom-call | tf_op jit(solution)/shard_map/pack_kv/pallas_call | solution.py:50
  2.5 0.7 collective-permute-start.17
  3.1 1.1 collective-permute-start.18
  4.3 2.1 %collective-permute-start.19 = (bf16[2,2,96,128]{3,2,1,0:T(8,128)(2,1)}, bf16[2,2,96,128]{3,2,1,0:T(8,128)(2,1)S(1)}, u32[]{:S(2)}, u32[]{:S(2)}) collective-permute-start(bf16[2,2,96,128]{3,2,1,0:T(8,128)(2,1)} %get-tuple-element.46), channel_id=1, source_target_pairs={{0,17},{1,16},{2,19},{3,18},{4,21},{5,20},{6,23},{7,22},{8,25},{9,... | collective-permute-start | bytes 294920 | tf_op jit(solution)/shard_map/ppermute | solution.py:265
  6.3 2.8 %collective-permute-done.18 = bf16[2,2,96,128]{3,2,1,0:T(8,128)(2,1)S(1)} collective-permute-done((bf16[2,2,96,128]{3,2,1,0:T(8,128)(2,1)}, bf16[2,2,96,128]{3,2,1,0:T(8,128)(2,1)S(1)}, u32[]{:S(2)}, u32[]{:S(2)}) %collective-permute-start.18) | collective-permute-done | bytes 98336 | tf_op jit(solution)/shard_map/ppermute | solution.py:265
  9.2 2.3 %collective-permute-done.19 = bf16[2,2,96,128]{3,2,1,0:T(8,128)(2,1)S(1)} collective-permute-done((bf16[2,2,96,128]{3,2,1,0:T(8,128)(2,1)}, bf16[2,2,96,128]{3,2,1,0:T(8,128)(2,1)S(1)}, u32[]{:S(2)}, u32[]{:S(2)}) %collective-permute-start.19) | collective-permute-done | bytes 98336 | tf_op jit(solution)/shard_map/ppermute | solution.py:265
  11.5 0.9 pad_maximum_fusion.1.refs_6_.refs_11_
  12.4 1.7 %collective-permute-start.20 = (bf16[2,4,2,96,128]{4,3,2,1,0:T(8,128)(2,1)S(1)}, bf16[2,4,2,96,128]{4,3,2,1,0:T(8,128)(2,1)S(1)}, u32[]{:S(2)}, u32[]{:S(2)}) collective-permute-start(bf16[2,4,2,96,128]{4,3,2,1,0:T(8,128)(2,1)S(1)} %pad_maximum_fusion.1.refs_6_.refs_11_), channel_id=1, source_target_pairs={{0,2},{1,3},{2,4},{3,5},{4,6},{5,7},{6,8},{7,9},{8,10},{9,11},{10,... | collective-permute-start | bytes 1179656 | tf_op jit(solution)/shard_map/ppermute | solution.py:265
  14.2 4.0 %collective-permute-start.23 = (bf16[2,4,2,96,128]{4,3,2,1,0:T(8,128)(2,1)S(1)}, bf16[2,4,2,96,128]{4,3,2,1,0:T(8,128)(2,1)S(1)}, u32[]{:S(2)}, u32[]{:S(2)}) collective-permute-start(bf16[2,4,2,96,128]{4,3,2,1,0:T(8,128)(2,1)S(1)} %pad_maximum_fusion.1.refs_6_.refs_11_), channel_id=1, source_target_pairs={{0,14},{1,15},{2,0},{3,1},{4,2},{5,3},{6,4},{7,5},{8,6},{9,7},{10,... | collective-permute-start | bytes 1179656 | tf_op jit(solution)/shard_map/ppermute | solution.py:265
  18.2 1.8 %pack_kv.2 = (bf16[2,2,96,128]{3,2,1,0:T(8,128)(2,1)}, bf16[2,2,96,128]{3,2,1,0:T(8,128)(2,1)}, bf16[2,2,96,128]{3,2,1,0:T(8,128)(2,1)}, bf16[2,2,96,128]{3,2,1,0:T(8,128)(2,1)}) custom-call(s32[1]{0:T(128)} %bitcast.place_ref.refs_0_, bf16[2,64,1024]{2,1,0:T(8,128)(2,1)} %ck.5, bf16[2,64,1024]{2,1,0:T(8,128)(2,1)} %cv.3, bf16[2,32,1024]{2,1,0:T(8,128)(2,1)} %sk.5, ...), custom_call_target="tpu_custom_call" | custom-call | tf_op jit(solution)/shard_map/pack_kv/pallas_call | solution.py:50
  20.5 1.3 %collective-permute-start.4 = (bf16[2,2,96,128]{3,2,1,0:T(8,128)(2,1)}, bf16[2,2,96,128]{3,2,1,0:T(8,128)(2,1)S(1)}, u32[]{:S(2)}, u32[]{:S(2)}) collective-permute-start(bf16[2,2,96,128]{3,2,1,0:T(8,128)(2,1)} %get-tuple-element.35), channel_id=1, source_target_pairs={{0,16},{1,17},{2,18},{3,19},{4,20},{5,21},{6,22},{7,23},{8,24},{9,... | collective-permute-start | bytes 294920 | tf_op jit(solution)/shard_map/ppermute | solution.py:265
  21.8 1.9 %collective-permute-start.5 = (bf16[2,2,96,128]{3,2,1,0:T(8,128)(2,1)}, bf16[2,2,96,128]{3,2,1,0:T(8,128)(2,1)S(1)}, u32[]{:S(2)}, u32[]{:S(2)}) collective-permute-start(bf16[2,2,96,128]{3,2,1,0:T(8,128)(2,1)} %get-tuple-element.36), channel_id=1, source_target_pairs={{0,17},{1,16},{2,19},{3,18},{4,21},{5,20},{6,23},{7,22},{8,25},{9,... | collective-permute-start | bytes 294920 | tf_op jit(solution)/shard_map/ppermute | solution.py:265
  23.7 2.8 %collective-permute-done.4 = bf16[2,2,96,128]{3,2,1,0:T(8,128)(2,1)S(1)} collective-permute-done((bf16[2,2,96,128]{3,2,1,0:T(8,128)(2,1)}, bf16[2,2,96,128]{3,2,1,0:T(8,128)(2,1)S(1)}, u32[]{:S(2)}, u32[]{:S(2)}) %collective-permute-start.4) | collective-permute-done | bytes 98336 | tf_op jit(solution)/shard_map/ppermute | solution.py:265
  26.5 2.3 %collective-permute-done.5 = bf16[2,2,96,128]{3,2,1,0:T(8,128)(2,1)S(1)} collective-permute-done((bf16[2,2,96,128]{3,2,1,0:T(8,128)(2,1)}, bf16[2,2,96,128]{3,2,1,0:T(8,128)(2,1)S(1)}, u32[]{:S(2)}, u32[]{:S(2)}) %collective-permute-start.5) | collective-permute-done | bytes 98336 | tf_op jit(solution)/shard_map/ppermute | solution.py:265
  28.8 0.9 pad_maximum_fusion.refs_6_.refs_11_
  29.8 1.7 %collective-permute-start.9 = (bf16[2,4,2,96,128]{4,3,2,1,0:T(8,128)(2,1)S(1)}, bf16[2,4,2,96,128]{4,3,2,1,0:T(8,128)(2,1)S(1)}, u32[]{:S(2)}, u32[]{:S(2)}) collective-permute-start(bf16[2,4,2,96,128]{4,3,2,1,0:T(8,128)(2,1)S(1)} %pad_maximum_fusion.refs_6_.refs_11_), channel_id=1, source_target_pairs={{0,14},{1,15},{2,0},{3,1},{4,2},{5,3},{6,4},{7,5},{8,6},{9,7},{10,... | collective-permute-start | bytes 1179656 | tf_op jit(solution)/shard_map/ppermute | solution.py:265
  31.6 2.7 %collective-permute-start.24 = (bf16[2,4,2,96,128]{4,3,2,1,0:T(8,128)(2,1)S(1)}, bf16[2,4,2,96,128]{4,3,2,1,0:T(8,128)(2,1)}, u32[]{:S(2)}, u32[]{:S(2)}) collective-permute-start(bf16[2,4,2,96,128]{4,3,2,1,0:T(8,128)(2,1)S(1)} %collective-permute-done.23.refs_8_.refs_13_), channel_id=1, source_target_pairs={{0,14},{1,15},{2,0},{3,1},{4,2},{5,3},{6,4},{7,5},{8,6},{9,7},{10,... | collective-permute-start | bytes 1179656 | tf_op jit(solution)/shard_map/ppermute | solution.py:265
  34.3 6.1 %collective-permute-done.9.refs_8_.refs_13_ = bf16[2,4,2,96,128]{4,3,2,1,0:T(8,128)(2,1)S(1)} collective-permute-done((bf16[2,4,2,96,128]{4,3,2,1,0:T(8,128)(2,1)S(1)}, bf16[2,4,2,96,128]{4,3,2,1,0:T(8,128)(2,1)S(1)}, u32[]{:S(2)}, u32[]{:S(2)}) %collective-permute-start.9) | collective-permute-done | bytes 393248 | tf_op jit(solution)/shard_map/ppermute | solution.py:265
  40.3 2.9 %collective-permute-start.10 = (bf16[2,4,2,96,128]{4,3,2,1,0:T(8,128)(2,1)S(1)}, bf16[2,4,2,96,128]{4,3,2,1,0:T(8,128)(2,1)}, u32[]{:S(2)}, u32[]{:S(2)}) collective-permute-start(bf16[2,4,2,96,128]{4,3,2,1,0:T(8,128)(2,1)S(1)} %collective-permute-done.9.refs_8_.refs_13_), channel_id=1, source_target_pairs={{0,14},{1,15},{2,0},{3,1},{4,2},{5,3},{6,4},{7,5},{8,6},{9,7},{10,... | collective-permute-start | bytes 1179656 | tf_op jit(solution)/shard_map/ppermute | solution.py:265
  43.2 8.1 %collective-permute-done.21.refs_9_.refs_14_ = bf16[2,4,2,96,128]{4,3,2,1,0:T(8,128)(2,1)S(1)} collective-permute-done((bf16[2,4,2,96,128]{4,3,2,1,0:T(8,128)(2,1)S(1)}, bf16[2,4,2,96,128]{4,3,2,1,0:T(8,128)(2,1)S(1)}, u32[]{:S(2)}, u32[]{:S(2)}) %collective-permute-start.21) | collective-permute-done | bytes 393248 | tf_op jit(solution)/shard_map/ppermute | solution.py:265
  51.4 2.7 %collective-permute-start.25 = (bf16[2,4,2,96,128]{4,3,2,1,0:T(8,128)(2,1)}, bf16[2,4,2,96,128]{4,3,2,1,0:T(8,128)(2,1)S(1)}, u32[]{:S(2)}, u32[]{:S(2)}) collective-permute-start(bf16[2,4,2,96,128]{4,3,2,1,0:T(8,128)(2,1)} %collective-permute-done.24.refs_10_.refs_15_), channel_id=1, source_target_pairs={{0,14},{1,15},{2,0},{3,1},{4,2},{5,3},{6,4},{7,5},{8,6},{9,7},{10,... | collective-permute-start | bytes 1179656 | tf_op jit(solution)/shard_map/ppermute | solution.py:265
  54.0 2.1 %pack_q.1 = (bf16[2,2,256,128]{3,2,1,0:T(8,128)(2,1)}, bf16[2,2,256,128]{3,2,1,0:T(8,128)(2,1)}, bf16[2,2,256,128]{3,2,1,0:T(8,128)(2,1)}, bf16[2,2,256,128]{3,2,1,0:T(8,128)(2,1)}) custom-call(s32[1]{0:T(128)} %bitcast.place_ref.refs_0_, bf16[2,32,8192]{2,1,0:T(8,128)(2,1)} %q.1), custom_call_target="tpu_custom_call" | custom-call | tf_op jit(solution)/shard_map/pack_q/pallas_call | solution.py:72
  56.2 2.8 %collective-permute-start = (bf16[2,2,256,128]{3,2,1,0:T(8,128)(2,1)}, bf16[2,2,256,128]{3,2,1,0:T(8,128)(2,1)S(1)}, u32[]{:S(2)}, u32[]{:S(2)}) collective-permute-start(bf16[2,2,256,128]{3,2,1,0:T(8,128)(2,1)} %get-tuple-element.30), channel_id=1, source_target_pairs={{0,1},{1,0},{2,3},{3,2},{4,5},{5,4},{6,7},{7,6},{8,9},{9,8},{10,11... | collective-permute-start | bytes 786440 | tf_op jit(solution)/shard_map/ppermute | solution.py:265
  59.0 1.6 %collective-permute-start.1 = (bf16[2,2,256,128]{3,2,1,0:T(8,128)(2,1)}, bf16[2,2,256,128]{3,2,1,0:T(8,128)(2,1)S(1)}, u32[]{:S(2)}, u32[]{:S(2)}) collective-permute-start(bf16[2,2,256,128]{3,2,1,0:T(8,128)(2,1)} %get-tuple-element.31), channel_id=1, source_target_pairs={{0,16},{1,17},{2,18},{3,19},{4,20},{5,21},{6,22},{7,23},{8,24},{9,... | collective-permute-start | bytes 786440 | tf_op jit(solution)/shard_map/ppermute | solution.py:265
  60.6 3.0 %collective-permute-start.2 = (bf16[2,2,256,128]{3,2,1,0:T(8,128)(2,1)}, bf16[2,2,256,128]{3,2,1,0:T(8,128)(2,1)S(1)}, u32[]{:S(2)}, u32[]{:S(2)}) collective-permute-start(bf16[2,2,256,128]{3,2,1,0:T(8,128)(2,1)} %get-tuple-element.32), channel_id=1, source_target_pairs={{0,17},{1,16},{2,19},{3,18},{4,21},{5,20},{6,23},{7,22},{8,25},{9,... | collective-permute-start | bytes 786440 | tf_op jit(solution)/shard_map/ppermute | solution.py:265
  63.6 4.6 %collective-permute-done.22.refs_6_.refs_9_ = bf16[2,4,2,96,128]{4,3,2,1,0:T(8,128)(2,1)S(1)} collective-permute-done((bf16[2,4,2,96,128]{4,3,2,1,0:T(8,128)(2,1)S(1)}, bf16[2,4,2,96,128]{4,3,2,1,0:T(8,128)(2,1)S(1)}, u32[]{:S(2)}, u32[]{:S(2)}) %collective-permute-start.22) | collective-permute-done | bytes 393248 | tf_op jit(solution)/shard_map/ppermute | solution.py:265
  68.2 2.7 %collective-permute-start.11 = (bf16[2,4,2,96,128]{4,3,2,1,0:T(8,128)(2,1)}, bf16[2,4,2,96,128]{4,3,2,1,0:T(8,128)(2,1)S(1)}, u32[]{:S(2)}, u32[]{:S(2)}) collective-permute-start(bf16[2,4,2,96,128]{4,3,2,1,0:T(8,128)(2,1)} %collective-permute-done.10.refs_10_.refs_15_), channel_id=1, source_target_pairs={{0,14},{1,15},{2,0},{3,1},{4,2},{5,3},{6,4},{7,5},{8,6},{9,7},{10,... | collective-permute-start | bytes 1179656 | tf_op jit(solution)/shard_map/ppermute | solution.py:265
  71.0 0.7 slice.18
  71.7 0.7 slice.19
  72.5 2.6 %collective-permute-start.27 = (bf16[1,4,2,96,128]{4,3,2,1,0:T(8,128)(2,1)}, bf16[1,4,2,96,128]{4,3,2,1,0:T(8,128)(2,1)S(1)}, u32[]{:S(2)}, u32[]{:S(2)}) collective-permute-start(bf16[1,4,2,96,128]{4,3,2,1,0:T(8,128)(2,1)} %slice.19), channel_id=1, source_target_pairs={{0,14},{1,15},{2,0},{3,1},{4,2},{5,3},{6,4},{7,5},{8,6},{9,7},{10,... | collective-permute-start | bytes 589832 | tf_op jit(solution)/shard_map/ppermute | solution.py:265
  75.2 0.7 copy-done.6
  75.9 8.6 %attend.6 = (f32[2,1024,256]{2,1,0:T(8,128)}, f32[2,1024,128]{2,1,0:T(8,128)}) custom-call(s32[1]{0:T(128)} %bitcast.place_ref.refs_0_, s32[2]{0:T(128)} %len_ref.1, bf16[2,2,256,128]{3,2,1,0:T(8,128)(2,1)} %get-tuple-element.29.refs_2_, bf16[2,2,256,128]{3,2,1,0:T(8,128)(2,1)} %copy-done.4, bf16[2,2,256,128]{3,2,1,0:T(8,128)(2,1)} %copy-done.5, ...), custom_call_target="tpu_custom_call" | custom-call | flops 2013265920 | bytes 4194304 | tf_op jit(solution)/shard_map/attend/pallas_call | solution.py:252
  84.6 2.7 %collective-permute-start.13 = (bf16[1,4,2,96,128]{4,3,2,1,0:T(8,128)(2,1)S(1)}, bf16[1,4,2,96,128]{4,3,2,1,0:T(8,128)(2,1)S(1)}, u32[]{:S(2)}, u32[]{:S(2)}) collective-permute-start(bf16[1,4,2,96,128]{4,3,2,1,0:T(8,128)(2,1)S(1)} %slice.17), channel_id=1, source_target_pairs={{0,14},{1,15},{2,0},{3,1},{4,2},{5,3},{6,4},{7,5},{8,6},{9,7},{10,... | collective-permute-start | bytes 589832 | tf_op jit(solution)/shard_map/ppermute | solution.py:265
  87.4 0.7 copy-done.11
  88.1 6.3 %attend.7 = (bf16[2,256,128]{2,1,0:T(8,128)(2,1)}, bf16[2,256,128]{2,1,0:T(8,128)(2,1)}, bf16[2,256,128]{2,1,0:T(8,128)(2,1)}, bf16[2,256,128]{2,1,0:T(8,128)(2,1)}) custom-call(s32[1]{0:T(128)} %bitcast.place_ref.refs_0_, s32[2]{0:T(128)} %len_ref.1, bf16[2,2,256,128]{3,2,1,0:T(8,128)(2,1)} %get-tuple-element.29.refs_2_, ...), custom_call_target="tpu_custom_call" | custom-call | flops 1207959552 | bytes 4194304 | tf_op jit(solution)/shard_map/attend/pallas_call | solution.py:252
  94.5 3.3 %collective-permute-start.28 = (bf16[2,256,128]{2,1,0:T(8,128)(2,1)}, bf16[2,256,128]{2,1,0:T(8,128)(2,1)S(1)}, u32[]{:S(2)}, u32[]{:S(2)}) collective-permute-start(bf16[2,256,128]{2,1,0:T(8,128)(2,1)} %get-tuple-element.50), channel_id=1, source_target_pairs={{0,1},{1,0},{2,3},{3,2},{4,5},{5,4},{6,7},{7,6},{8,9},{9,8},{10,11... | collective-permute-start | bytes 393224 | tf_op jit(solution)/shard_map/ppermute | solution.py:265
  97.8 8.6 %attend.4 = (f32[2,1024,256]{2,1,0:T(8,128)}, f32[2,1024,128]{2,1,0:T(8,128)}) custom-call(s32[1]{0:T(128)} %bitcast.place_ref.refs_0_, s32[2]{0:T(128)} %len_ref.1, bf16[2,2,256,128]{3,2,1,0:T(8,128)(2,1)} %get-tuple-element.29.refs_2_, bf16[2,2,256,128]{3,2,1,0:T(8,128)(2,1)} %copy-done.4, bf16[2,2,256,128]{3,2,1,0:T(8,128)(2,1)} %copy-done.5, ...), custom_call_target="tpu_custom_call" | custom-call | flops 2013265920 | bytes 4194304 | tf_op jit(solution)/shard_map/attend/pallas_call | solution.py:252
  106.4 1.5 %collective-permute-start.29 = (bf16[2,256,128]{2,1,0:T(8,128)(2,1)S(1)}, bf16[2,256,128]{2,1,0:T(8,128)(2,1)S(1)}, u32[]{:S(2)}, u32[]{:S(2)}) collective-permute-start(bf16[2,256,128]{2,1,0:T(8,128)(2,1)S(1)} %copy-done.25), channel_id=1, source_target_pairs={{0,16},{1,17},{2,18},{3,19},{4,20},{5,21},{6,22},{7,23},{8,24},{9,... | collective-permute-start | bytes 393224 | tf_op jit(solution)/shard_map/ppermute | solution.py:265
  107.8 1.8 %collective-permute-start.30 = (bf16[2,256,128]{2,1,0:T(8,128)(2,1)S(1)}, bf16[2,256,128]{2,1,0:T(8,128)(2,1)S(1)}, u32[]{:S(2)}, u32[]{:S(2)}) collective-permute-start(bf16[2,256,128]{2,1,0:T(8,128)(2,1)S(1)} %copy-done.24), channel_id=1, source_target_pairs={{0,17},{1,16},{2,19},{3,18},{4,21},{5,20},{6,23},{7,22},{8,25},{9,... | collective-permute-start | bytes 393224 | tf_op jit(solution)/shard_map/ppermute | solution.py:265
  109.6 0.7 copy-done.9
  110.4 6.3 %attend.5 = (bf16[2,256,128]{2,1,0:T(8,128)(2,1)}, bf16[2,256,128]{2,1,0:T(8,128)(2,1)}, bf16[2,256,128]{2,1,0:T(8,128)(2,1)}, bf16[2,256,128]{2,1,0:T(8,128)(2,1)}) custom-call(s32[1]{0:T(128)} %bitcast.place_ref.refs_0_, s32[2]{0:T(128)} %len_ref.1, bf16[2,2,256,128]{3,2,1,0:T(8,128)(2,1)} %get-tuple-element.29.refs_2_, ...), custom_call_target="tpu_custom_call" | custom-call | flops 1207959552 | bytes 4194304 | tf_op jit(solution)/shard_map/attend/pallas_call | solution.py:252
  117.0 1.4 %collective-permute-start.15 = (bf16[2,256,128]{2,1,0:T(8,128)(2,1)}, bf16[2,256,128]{2,1,0:T(8,128)(2,1)S(1)}, u32[]{:S(2)}, u32[]{:S(2)}) collective-permute-start(bf16[2,256,128]{2,1,0:T(8,128)(2,1)} %get-tuple-element.41), channel_id=1, source_target_pairs={{0,16},{1,17},{2,18},{3,19},{4,20},{5,21},{6,22},{7,23},{8,24},{9,... | collective-permute-start | bytes 393224 | tf_op jit(solution)/shard_map/ppermute | solution.py:265
  118.4 2.1 %collective-permute-start.16 = (bf16[2,256,128]{2,1,0:T(8,128)(2,1)}, bf16[2,256,128]{2,1,0:T(8,128)(2,1)S(1)}, u32[]{:S(2)}, u32[]{:S(2)}) collective-permute-start(bf16[2,256,128]{2,1,0:T(8,128)(2,1)} %get-tuple-element.42), channel_id=1, source_target_pairs={{0,17},{1,16},{2,19},{3,18},{4,21},{5,20},{6,23},{7,22},{8,25},{9,... | collective-permute-start | bytes 393224 | tf_op jit(solution)/shard_map/ppermute | solution.py:265
  120.5 1.9 %page_bounds.1 = (bf16[2,4,2048]{2,1,0:T(4,128)(2,1)}, bf16[2,2,2048]{2,1,0:T(2,128)(2,1)}) custom-call(s32[1]{0:T(128)} %bitcast.place_ref.refs_0_, s32[2]{0:T(128)} %len_ref.1, bf16[2,64,1024]{2,1,0:T(8,128)(2,1)} %ck.5, bf16[2,32,1024]{2,1,0:T(8,128)(2,1)} %sk.5), custom_call_target="tpu_custom_call" | custom-call | tf_op jit(solution)/shard_map/page_bounds/pallas_call | solution.py:124
  122.4 1.1 collective-permute-done.15.refs_2_
  123.4 3.3 %collective-permute-done.16.refs_3_ = bf16[2,256,128]{2,1,0:T(8,128)(2,1)S(1)} collective-permute-done((bf16[2,256,128]{2,1,0:T(8,128)(2,1)}, bf16[2,256,128]{2,1,0:T(8,128)(2,1)S(1)}, u32[]{:S(2)}, u32[]{:S(2)}) %collective-permute-start.16) | collective-permute-done | bytes 131104 | tf_op jit(solution)/shard_map/ppermute | solution.py:265
  126.8 0.6 copy-done.18
  127.4 2.5 %unpack_out.1 = bf16[2,32,8192]{2,1,0:T(8,128)(2,1)} custom-call(s32[1]{0:T(128)} %bitcast.place_ref.refs_0_, bf16[2,256,128]{2,1,0:T(8,128)(2,1)} %get-tuple-element.39.refs_0_, bf16[2,256,128]{2,1,0:T(8,128)(2,1)} %copy-done.16, bf16[2,256,128]{2,1,0:T(8,128)(2,1)} %copy-done.17, bf16[2,256,128]{2,1,0:T(8,128)(2,1)} %copy-done.18, ...), custom_call_target="tpu_custom_call" | custom-call | tf_op jit(solution)/shard_map/unpack_out/pallas_call | solution.py:96
  (81 shorter events, 1.3 us)
Async XLA Ops:
  2.5 3.9 %collective-permute-start.17 = (bf16[2,2,96,128]{3,2,1,0:T(8,128)(2,1)}, bf16[2,2,96,128]{3,2,1,0:T(8,128)(2,1)S(1)}, u32[]{:S(2)}, u32[]{:S(2)}) collective-permute-start(bf16[2,2,96,128]{3,2,1,0:T(8,128)(2,1)} %get-tuple-element.44), channel_id=1, source_target_pairs={{0,1},{1,0},{2,3},{3,2},{4,5},{5,4},{6,7},{7,6},{8,9},{9,8},{10,11... | collective-permute-start | bytes 294920 | tf_op jit(solution)/shard_map/ppermute | solution.py:265
  3.1 6.0 %collective-permute-start.18 = (bf16[2,2,96,128]{3,2,1,0:T(8,128)(2,1)}, bf16[2,2,96,128]{3,2,1,0:T(8,128)(2,1)S(1)}, u32[]{:S(2)}, u32[]{:S(2)}) collective-permute-start(bf16[2,2,96,128]{3,2,1,0:T(8,128)(2,1)} %get-tuple-element.45), channel_id=1, source_target_pairs={{0,16},{1,17},{2,18},{3,19},{4,20},{5,21},{6,22},{7,23},{8,24},{9,... | collective-permute-start | bytes 294920 | tf_op jit(solution)/shard_map/ppermute | solution.py:265
  4.3 7.2 %collective-permute-start.19 = (bf16[2,2,96,128]{3,2,1,0:T(8,128)(2,1)}, bf16[2,2,96,128]{3,2,1,0:T(8,128)(2,1)S(1)}, u32[]{:S(2)}, u32[]{:S(2)}) collective-permute-start(bf16[2,2,96,128]{3,2,1,0:T(8,128)(2,1)} %get-tuple-element.46), channel_id=1, source_target_pairs={{0,17},{1,16},{2,19},{3,18},{4,21},{5,20},{6,23},{7,22},{8,25},{9,... | collective-permute-start | bytes 294920 | tf_op jit(solution)/shard_map/ppermute | solution.py:265
  12.4 62.7 %copy-start.8 = (bf16[2,4,2,96,128]{4,3,2,1,0:T(8,128)(2,1)}, bf16[2,4,2,96,128]{4,3,2,1,0:T(8,128)(2,1)S(1)}, u32[]{:S(2)}) copy-start(bf16[2,4,2,96,128]{4,3,2,1,0:T(8,128)(2,1)S(1)} %pad_maximum_fusion.1.refs_6_.refs_11_) | copy-start | bytes 1179652
  12.4 19.1 %collective-permute-start.20 = (bf16[2,4,2,96,128]{4,3,2,1,0:T(8,128)(2,1)S(1)}, bf16[2,4,2,96,128]{4,3,2,1,0:T(8,128)(2,1)S(1)}, u32[]{:S(2)}, u32[]{:S(2)}) collective-permute-start(bf16[2,4,2,96,128]{4,3,2,1,0:T(8,128)(2,1)S(1)} %pad_maximum_fusion.1.refs_6_.refs_11_), channel_id=1, source_target_pairs={{0,2},{1,3},{2,4},{3,5},{4,6},{5,7},{6,8},{7,9},{8,10},{9,11},{10,... | collective-permute-start | bytes 1179656 | tf_op jit(solution)/shard_map/ppermute | solution.py:265
  14.2 17.5 %collective-permute-start.23 = (bf16[2,4,2,96,128]{4,3,2,1,0:T(8,128)(2,1)S(1)}, bf16[2,4,2,96,128]{4,3,2,1,0:T(8,128)(2,1)S(1)}, u32[]{:S(2)}, u32[]{:S(2)}) collective-permute-start(bf16[2,4,2,96,128]{4,3,2,1,0:T(8,128)(2,1)S(1)} %pad_maximum_fusion.1.refs_6_.refs_11_), channel_id=1, source_target_pairs={{0,14},{1,15},{2,0},{3,1},{4,2},{5,3},{6,4},{7,5},{8,6},{9,7},{10,... | collective-permute-start | bytes 1179656 | tf_op jit(solution)/shard_map/ppermute | solution.py:265
  20.0 3.6 %collective-permute-start.3 = (bf16[2,2,96,128]{3,2,1,0:T(8,128)(2,1)}, bf16[2,2,96,128]{3,2,1,0:T(8,128)(2,1)S(1)}, u32[]{:S(2)}, u32[]{:S(2)}) collective-permute-start(bf16[2,2,96,128]{3,2,1,0:T(8,128)(2,1)} %get-tuple-element.34), channel_id=1, source_target_pairs={{0,1},{1,0},{2,3},{3,2},{4,5},{5,4},{6,7},{7,6},{8,9},{9,8},{10,11... | collective-permute-start | bytes 294920 | tf_op jit(solution)/shard_map/ppermute | solution.py:265
  20.5 6.0 %collective-permute-start.4 = (bf16[2,2,96,128]{3,2,1,0:T(8,128)(2,1)}, bf16[2,2,96,128]{3,2,1,0:T(8,128)(2,1)S(1)}, u32[]{:S(2)}, u32[]{:S(2)}) collective-permute-start(bf16[2,2,96,128]{3,2,1,0:T(8,128)(2,1)} %get-tuple-element.35), channel_id=1, source_target_pairs={{0,16},{1,17},{2,18},{3,19},{4,20},{5,21},{6,22},{7,23},{8,24},{9,... | collective-permute-start | bytes 294920 | tf_op jit(solution)/shard_map/ppermute | solution.py:265
  21.8 7.0 %collective-permute-start.5 = (bf16[2,2,96,128]{3,2,1,0:T(8,128)(2,1)}, bf16[2,2,96,128]{3,2,1,0:T(8,128)(2,1)S(1)}, u32[]{:S(2)}, u32[]{:S(2)}) collective-permute-start(bf16[2,2,96,128]{3,2,1,0:T(8,128)(2,1)} %get-tuple-element.36), channel_id=1, source_target_pairs={{0,17},{1,16},{2,19},{3,18},{4,21},{5,20},{6,23},{7,22},{8,25},{9,... | collective-permute-start | bytes 294920 | tf_op jit(solution)/shard_map/ppermute | solution.py:265
  29.8 54.7 %copy-start.7 = (bf16[2,4,2,96,128]{4,3,2,1,0:T(8,128)(2,1)}, bf16[2,4,2,96,128]{4,3,2,1,0:T(8,128)(2,1)S(1)}, u32[]{:S(2)}) copy-start(bf16[2,4,2,96,128]{4,3,2,1,0:T(8,128)(2,1)S(1)} %pad_maximum_fusion.refs_6_.refs_11_) | copy-start | bytes 1179652
  29.8 10.6 %collective-permute-start.9 = (bf16[2,4,2,96,128]{4,3,2,1,0:T(8,128)(2,1)S(1)}, bf16[2,4,2,96,128]{4,3,2,1,0:T(8,128)(2,1)S(1)}, u32[]{:S(2)}, u32[]{:S(2)}) collective-permute-start(bf16[2,4,2,96,128]{4,3,2,1,0:T(8,128)(2,1)S(1)} %pad_maximum_fusion.refs_6_.refs_11_), channel_id=1, source_target_pairs={{0,14},{1,15},{2,0},{3,1},{4,2},{5,3},{6,4},{7,5},{8,6},{9,7},{10,... | collective-permute-start | bytes 1179656 | tf_op jit(solution)/shard_map/ppermute | solution.py:265
  31.5 11.7 %collective-permute-start.6 = (bf16[2,4,2,96,128]{4,3,2,1,0:T(8,128)(2,1)S(1)}, bf16[2,4,2,96,128]{4,3,2,1,0:T(8,128)(2,1)S(1)}, u32[]{:S(2)}, u32[]{:S(2)}) collective-permute-start(bf16[2,4,2,96,128]{4,3,2,1,0:T(8,128)(2,1)S(1)} %pad_maximum_fusion.refs_6_.refs_11_), channel_id=1, source_target_pairs={{0,2},{1,3},{2,4},{3,5},{4,6},{5,7},{6,8},{7,9},{8,10},{9,11},{10,... | collective-permute-start | bytes 1179656 | tf_op jit(solution)/shard_map/ppermute | solution.py:265
  31.5 36.7 %copy-start.21 = (bf16[2,4,2,96,128]{4,3,2,1,0:T(8,128)(2,1)}, bf16[2,4,2,96,128]{4,3,2,1,0:T(8,128)(2,1)S(1)}, u32[]{:S(2)}) copy-start(bf16[2,4,2,96,128]{4,3,2,1,0:T(8,128)(2,1)S(1)} %collective-permute-done.20.refs_7_.refs_12_) | copy-start | bytes 1179652
  31.5 19.8 %collective-permute-start.21 = (bf16[2,4,2,96,128]{4,3,2,1,0:T(8,128)(2,1)S(1)}, bf16[2,4,2,96,128]{4,3,2,1,0:T(8,128)(2,1)S(1)}, u32[]{:S(2)}, u32[]{:S(2)}) collective-permute-start(bf16[2,4,2,96,128]{4,3,2,1,0:T(8,128)(2,1)S(1)} %collective-permute-done.20.refs_7_.refs_12_), channel_id=1, source_target_pairs={{0,2},{1,3},{2,4},{3,5},{4,6},{5,7},{6,8},{7,9},{8,10},{9,11},{10,... | collective-permute-start | bytes 1179656 | tf_op jit(solution)/shard_map/ppermute | solution.py:265
  31.6 19.7 %copy-start.22 = (bf16[2,4,2,96,128]{4,3,2,1,0:T(8,128)(2,1)}, bf16[2,4,2,96,128]{4,3,2,1,0:T(8,128)(2,1)S(1)}, u32[]{:S(2)}) copy-start(bf16[2,4,2,96,128]{4,3,2,1,0:T(8,128)(2,1)S(1)} %collective-permute-done.23.refs_8_.refs_13_) | copy-start | bytes 1179652
  31.6 19.7 %collective-permute-start.24 = (bf16[2,4,2,96,128]{4,3,2,1,0:T(8,128)(2,1)S(1)}, bf16[2,4,2,96,128]{4,3,2,1,0:T(8,128)(2,1)}, u32[]{:S(2)}, u32[]{:S(2)}) collective-permute-start(bf16[2,4,2,96,128]{4,3,2,1,0:T(8,128)(2,1)S(1)} %collective-permute-done.23.refs_8_.refs_13_), channel_id=1, source_target_pairs={{0,14},{1,15},{2,0},{3,1},{4,2},{5,3},{6,4},{7,5},{8,6},{9,7},{10,... | collective-permute-start | bytes 1179656 | tf_op jit(solution)/shard_map/ppermute | solution.py:265
  40.3 18.6 %copy-start.19 = (bf16[2,4,2,96,128]{4,3,2,1,0:T(8,128)(2,1)}, bf16[2,4,2,96,128]{4,3,2,1,0:T(8,128)(2,1)S(1)}, u32[]{:S(2)}) copy-start(bf16[2,4,2,96,128]{4,3,2,1,0:T(8,128)(2,1)S(1)} %collective-permute-done.9.refs_8_.refs_13_) | copy-start | bytes 1179652
  40.3 18.6 %collective-permute-start.10 = (bf16[2,4,2,96,128]{4,3,2,1,0:T(8,128)(2,1)S(1)}, bf16[2,4,2,96,128]{4,3,2,1,0:T(8,128)(2,1)}, u32[]{:S(2)}, u32[]{:S(2)}) collective-permute-start(bf16[2,4,2,96,128]{4,3,2,1,0:T(8,128)(2,1)S(1)} %collective-permute-done.9.refs_8_.refs_13_), channel_id=1, source_target_pairs={{0,14},{1,15},{2,0},{3,1},{4,2},{5,3},{6,4},{7,5},{8,6},{9,7},{10,... | collective-permute-start | bytes 1179656 | tf_op jit(solution)/shard_map/ppermute | solution.py:265
  43.2 20.4 %copy-start.20 = (bf16[2,4,2,96,128]{4,3,2,1,0:T(8,128)(2,1)}, bf16[2,4,2,96,128]{4,3,2,1,0:T(8,128)(2,1)S(1)}, u32[]{:S(2)}) copy-start(bf16[2,4,2,96,128]{4,3,2,1,0:T(8,128)(2,1)S(1)} %collective-permute-done.6.refs_7_.refs_12_) | copy-start | bytes 1179652
  43.2 17.3 %collective-permute-start.7 = (bf16[2,4,2,96,128]{4,3,2,1,0:T(8,128)(2,1)S(1)}, bf16[2,4,2,96,128]{4,3,2,1,0:T(8,128)(2,1)}, u32[]{:S(2)}, u32[]{:S(2)}) collective-permute-start(bf16[2,4,2,96,128]{4,3,2,1,0:T(8,128)(2,1)S(1)} %collective-permute-done.6.refs_7_.refs_12_), channel_id=1, source_target_pairs={{0,2},{1,3},{2,4},{3,5},{4,6},{5,7},{6,8},{7,9},{8,10},{9,11},{10,... | collective-permute-start | bytes 1179656 | tf_op jit(solution)/shard_map/ppermute | solution.py:265
  51.4 21.0 %copy-start.23 = (bf16[2,4,2,96,128]{4,3,2,1,0:T(8,128)(2,1)}, bf16[2,4,2,96,128]{4,3,2,1,0:T(8,128)(2,1)S(1)}, u32[]{:S(2)}) copy-start(bf16[2,4,2,96,128]{4,3,2,1,0:T(8,128)(2,1)S(1)} %collective-permute-done.21.refs_9_.refs_14_) | copy-start | bytes 1179652
  51.4 16.9 %collective-permute-start.22 = (bf16[2,4,2,96,128]{4,3,2,1,0:T(8,128)(2,1)S(1)}, bf16[2,4,2,96,128]{4,3,2,1,0:T(8,128)(2,1)S(1)}, u32[]{:S(2)}, u32[]{:S(2)}) collective-permute-start(bf16[2,4,2,96,128]{4,3,2,1,0:T(8,128)(2,1)S(1)} %collective-permute-done.21.refs_9_.refs_14_), channel_id=1, source_target_pairs={{0,2},{1,3},{2,4},{3,5},{4,6},{5,7},{6,8},{7,9},{8,10},{9,11},{10,... | collective-permute-start | bytes 1179656 | tf_op jit(solution)/shard_map/ppermute | solution.py:265
  51.4 16.8 %collective-permute-start.25 = (bf16[2,4,2,96,128]{4,3,2,1,0:T(8,128)(2,1)}, bf16[2,4,2,96,128]{4,3,2,1,0:T(8,128)(2,1)S(1)}, u32[]{:S(2)}, u32[]{:S(2)}) collective-permute-start(bf16[2,4,2,96,128]{4,3,2,1,0:T(8,128)(2,1)} %collective-permute-done.24.refs_10_.refs_15_), channel_id=1, source_target_pairs={{0,14},{1,15},{2,0},{3,1},{4,2},{5,3},{6,4},{7,5},{8,6},{9,7},{10,... | collective-permute-start | bytes 1179656 | tf_op jit(solution)/shard_map/ppermute | solution.py:265
  56.2 16.2 %collective-permute-start = (bf16[2,2,256,128]{3,2,1,0:T(8,128)(2,1)}, bf16[2,2,256,128]{3,2,1,0:T(8,128)(2,1)S(1)}, u32[]{:S(2)}, u32[]{:S(2)}) collective-permute-start(bf16[2,2,256,128]{3,2,1,0:T(8,128)(2,1)} %get-tuple-element.30), channel_id=1, source_target_pairs={{0,1},{1,0},{2,3},{3,2},{4,5},{5,4},{6,7},{7,6},{8,9},{9,8},{10,11... | collective-permute-start | bytes 786440 | tf_op jit(solution)/shard_map/ppermute | solution.py:265
  59.0 13.5 %collective-permute-start.1 = (bf16[2,2,256,128]{3,2,1,0:T(8,128)(2,1)}, bf16[2,2,256,128]{3,2,1,0:T(8,128)(2,1)S(1)}, u32[]{:S(2)}, u32[]{:S(2)}) collective-permute-start(bf16[2,2,256,128]{3,2,1,0:T(8,128)(2,1)} %get-tuple-element.31), channel_id=1, source_target_pairs={{0,16},{1,17},{2,18},{3,19},{4,20},{5,21},{6,22},{7,23},{8,24},{9,... | collective-permute-start | bytes 786440 | tf_op jit(solution)/shard_map/ppermute | solution.py:265
  60.6 14.6 %collective-permute-start.2 = (bf16[2,2,256,128]{3,2,1,0:T(8,128)(2,1)}, bf16[2,2,256,128]{3,2,1,0:T(8,128)(2,1)S(1)}, u32[]{:S(2)}, u32[]{:S(2)}) collective-permute-start(bf16[2,2,256,128]{3,2,1,0:T(8,128)(2,1)} %get-tuple-element.32), channel_id=1, source_target_pairs={{0,17},{1,16},{2,19},{3,18},{4,21},{5,20},{6,23},{7,22},{8,25},{9,... | collective-permute-start | bytes 786440 | tf_op jit(solution)/shard_map/ppermute | solution.py:265
  68.2 16.2 %copy-start.2 = (bf16[2,4,2,96,128]{4,3,2,1,0:T(8,128)(2,1)}, bf16[2,4,2,96,128]{4,3,2,1,0:T(8,128)(2,1)S(1)}, u32[]{:S(2)}) copy-start(bf16[2,4,2,96,128]{4,3,2,1,0:T(8,128)(2,1)S(1)} %collective-permute-done.22.refs_6_.refs_9_) | copy-start | bytes 1179652
  68.2 16.2 %collective-permute-start.8 = (bf16[2,4,2,96,128]{4,3,2,1,0:T(8,128)(2,1)}, bf16[2,4,2,96,128]{4,3,2,1,0:T(8,128)(2,1)S(1)}, u32[]{:S(2)}, u32[]{:S(2)}) collective-permute-start(bf16[2,4,2,96,128]{4,3,2,1,0:T(8,128)(2,1)} %collective-permute-done.7.refs_9_.refs_14_), channel_id=1, source_target_pairs={{0,2},{1,3},{2,4},{3,5},{4,6},{5,7},{6,8},{7,9},{8,10},{9,11},{10,... | collective-permute-start | bytes 1179656 | tf_op jit(solution)/shard_map/ppermute | solution.py:265
  68.2 16.2 %copy-start.3 = (bf16[2,4,2,96,128]{4,3,2,1,0:T(8,128)(2,1)}, bf16[2,4,2,96,128]{4,3,2,1,0:T(8,128)(2,1)S(1)}, u32[]{:S(2)}) copy-start(bf16[2,4,2,96,128]{4,3,2,1,0:T(8,128)(2,1)S(1)} %collective-permute-done.25.refs_7_.refs_10_) | copy-start | bytes 1179652
  68.2 16.4 %collective-permute-start.11 = (bf16[2,4,2,96,128]{4,3,2,1,0:T(8,128)(2,1)}, bf16[2,4,2,96,128]{4,3,2,1,0:T(8,128)(2,1)S(1)}, u32[]{:S(2)}, u32[]{:S(2)}) collective-permute-start(bf16[2,4,2,96,128]{4,3,2,1,0:T(8,128)(2,1)} %collective-permute-done.10.refs_10_.refs_15_), channel_id=1, source_target_pairs={{0,14},{1,15},{2,0},{3,1},{4,2},{5,3},{6,4},{7,5},{8,6},{9,7},{10,... | collective-permute-start | bytes 1179656 | tf_op jit(solution)/shard_map/ppermute | solution.py:265
  72.4 15.0 %collective-permute-start.26 = (bf16[1,4,2,96,128]{4,3,2,1,0:T(8,128)(2,1)}, bf16[1,4,2,96,128]{4,3,2,1,0:T(8,128)(2,1)S(1)}, u32[]{:S(2)}, u32[]{:S(2)}) collective-permute-start(bf16[1,4,2,96,128]{4,3,2,1,0:T(8,128)(2,1)} %slice.18), channel_id=1, source_target_pairs={{0,2},{1,3},{2,4},{3,5},{4,6},{5,7},{6,8},{7,9},{8,10},{9,11},{10,... | collective-permute-start | bytes 589832 | tf_op jit(solution)/shard_map/ppermute | solution.py:265
  72.5 14.9 %collective-permute-start.27 = (bf16[1,4,2,96,128]{4,3,2,1,0:T(8,128)(2,1)}, bf16[1,4,2,96,128]{4,3,2,1,0:T(8,128)(2,1)S(1)}, u32[]{:S(2)}, u32[]{:S(2)}) collective-permute-start(bf16[1,4,2,96,128]{4,3,2,1,0:T(8,128)(2,1)} %slice.19), channel_id=1, source_target_pairs={{0,14},{1,15},{2,0},{3,1},{4,2},{5,3},{6,4},{7,5},{8,6},{9,7},{10,... | collective-permute-start | bytes 589832 | tf_op jit(solution)/shard_map/ppermute | solution.py:265
  84.5 10.0 %copy-start = (bf16[2,4,2,96,128]{4,3,2,1,0:T(8,128)(2,1)}, bf16[2,4,2,96,128]{4,3,2,1,0:T(8,128)(2,1)S(1)}, u32[]{:S(2)}) copy-start(bf16[2,4,2,96,128]{4,3,2,1,0:T(8,128)(2,1)S(1)} %collective-permute-done.8.refs_6_.refs_9_) | copy-start | bytes 1179652
  84.5 25.1 %collective-permute-start.12 = (bf16[1,4,2,96,128]{4,3,2,1,0:T(8,128)(2,1)S(1)}, bf16[1,4,2,96,128]{4,3,2,1,0:T(8,128)(2,1)S(1)}, u32[]{:S(2)}, u32[]{:S(2)}) collective-permute-start(bf16[1,4,2,96,128]{4,3,2,1,0:T(8,128)(2,1)S(1)} %slice.16), channel_id=1, source_target_pairs={{0,2},{1,3},{2,4},{3,5},{4,6},{5,7},{6,8},{7,9},{8,10},{9,11},{10,... | collective-permute-start | bytes 589832 | tf_op jit(solution)/shard_map/ppermute | solution.py:265
  84.6 9.9 %copy-start.1 = (bf16[2,4,2,96,128]{4,3,2,1,0:T(8,128)(2,1)}, bf16[2,4,2,96,128]{4,3,2,1,0:T(8,128)(2,1)S(1)}, u32[]{:S(2)}) copy-start(bf16[2,4,2,96,128]{4,3,2,1,0:T(8,128)(2,1)S(1)} %collective-permute-done.11.refs_7_.refs_10_) | copy-start | bytes 1179652
  84.6 25.0 %collective-permute-start.13 = (bf16[1,4,2,96,128]{4,3,2,1,0:T(8,128)(2,1)S(1)}, bf16[1,4,2,96,128]{4,3,2,1,0:T(8,128)(2,1)S(1)}, u32[]{:S(2)}, u32[]{:S(2)}) collective-permute-start(bf16[1,4,2,96,128]{4,3,2,1,0:T(8,128)(2,1)S(1)} %slice.17), channel_id=1, source_target_pairs={{0,14},{1,15},{2,0},{3,1},{4,2},{5,3},{6,4},{7,5},{8,6},{9,7},{10,... | collective-permute-start | bytes 589832 | tf_op jit(solution)/shard_map/ppermute | solution.py:265
  94.5 11.9 %copy-start.25 = (bf16[2,256,128]{2,1,0:T(8,128)(2,1)S(1)}, bf16[2,256,128]{2,1,0:T(8,128)(2,1)}, u32[]{:S(2)}) copy-start(bf16[2,256,128]{2,1,0:T(8,128)(2,1)} %get-tuple-element.51) | copy-start | bytes 393220
  94.5 13.3 %copy-start.24 = (bf16[2,256,128]{2,1,0:T(8,128)(2,1)S(1)}, bf16[2,256,128]{2,1,0:T(8,128)(2,1)}, u32[]{:S(2)}) copy-start(bf16[2,256,128]{2,1,0:T(8,128)(2,1)} %get-tuple-element.52) | copy-start | bytes 393220
  94.5 23.9 %collective-permute-start.28 = (bf16[2,256,128]{2,1,0:T(8,128)(2,1)}, bf16[2,256,128]{2,1,0:T(8,128)(2,1)S(1)}, u32[]{:S(2)}, u32[]{:S(2)}) collective-permute-start(bf16[2,256,128]{2,1,0:T(8,128)(2,1)} %get-tuple-element.50), channel_id=1, source_target_pairs={{0,1},{1,0},{2,3},{3,2},{4,5},{5,4},{6,7},{7,6},{8,9},{9,8},{10,11... | collective-permute-start | bytes 393224 | tf_op jit(solution)/shard_map/ppermute | solution.py:265
  106.4 16.0 %collective-permute-start.29 = (bf16[2,256,128]{2,1,0:T(8,128)(2,1)S(1)}, bf16[2,256,128]{2,1,0:T(8,128)(2,1)S(1)}, u32[]{:S(2)}, u32[]{:S(2)}) collective-permute-start(bf16[2,256,128]{2,1,0:T(8,128)(2,1)S(1)} %copy-done.25), channel_id=1, source_target_pairs={{0,16},{1,17},{2,18},{3,19},{4,20},{5,21},{6,22},{7,23},{8,24},{9,... | collective-permute-start | bytes 393224 | tf_op jit(solution)/shard_map/ppermute | solution.py:265
  107.8 14.5 %collective-permute-start.30 = (bf16[2,256,128]{2,1,0:T(8,128)(2,1)S(1)}, bf16[2,256,128]{2,1,0:T(8,128)(2,1)S(1)}, u32[]{:S(2)}, u32[]{:S(2)}) collective-permute-start(bf16[2,256,128]{2,1,0:T(8,128)(2,1)S(1)} %copy-done.24), channel_id=1, source_target_pairs={{0,17},{1,16},{2,19},{3,18},{4,21},{5,20},{6,23},{7,22},{8,25},{9,... | collective-permute-start | bytes 393224 | tf_op jit(solution)/shard_map/ppermute | solution.py:265
  116.7 5.6 %collective-permute-start.14 = (bf16[2,256,128]{2,1,0:T(8,128)(2,1)}, bf16[2,256,128]{2,1,0:T(8,128)(2,1)S(1)}, u32[]{:S(2)}, u32[]{:S(2)}) collective-permute-start(bf16[2,256,128]{2,1,0:T(8,128)(2,1)} %get-tuple-element.40), channel_id=1, source_target_pairs={{0,1},{1,0},{2,3},{3,2},{4,5},{5,4},{6,7},{7,6},{8,9},{9,8},{10,11... | collective-permute-start | bytes 393224 | tf_op jit(solution)/shard_map/ppermute | solution.py:265
  117.0 6.5 %collective-permute-start.15 = (bf16[2,256,128]{2,1,0:T(8,128)(2,1)}, bf16[2,256,128]{2,1,0:T(8,128)(2,1)S(1)}, u32[]{:S(2)}, u32[]{:S(2)}) collective-permute-start(bf16[2,256,128]{2,1,0:T(8,128)(2,1)} %get-tuple-element.41), channel_id=1, source_target_pairs={{0,16},{1,17},{2,18},{3,19},{4,20},{5,21},{6,22},{7,23},{8,24},{9,... | collective-permute-start | bytes 393224 | tf_op jit(solution)/shard_map/ppermute | solution.py:265
  118.4 8.4 %copy-start.13 = (bf16[2,256,128]{2,1,0:T(8,128)(2,1)}, bf16[2,256,128]{2,1,0:T(8,128)(2,1)S(1)}, u32[]{:S(2)}) copy-start(bf16[2,256,128]{2,1,0:T(8,128)(2,1)S(1)} %collective-permute-done.28.refs_5_) | copy-start | bytes 393220
  118.4 8.4 %collective-permute-start.16 = (bf16[2,256,128]{2,1,0:T(8,128)(2,1)}, bf16[2,256,128]{2,1,0:T(8,128)(2,1)S(1)}, u32[]{:S(2)}, u32[]{:S(2)}) collective-permute-start(bf16[2,256,128]{2,1,0:T(8,128)(2,1)} %get-tuple-element.42), channel_id=1, source_target_pairs={{0,17},{1,16},{2,19},{3,18},{4,21},{5,20},{6,23},{7,22},{8,25},{9,... | collective-permute-start | bytes 393224 | tf_op jit(solution)/shard_map/ppermute | solution.py:265
  122.3 4.4 %copy-start.14 = (bf16[2,256,128]{2,1,0:T(8,128)(2,1)}, bf16[2,256,128]{2,1,0:T(8,128)(2,1)S(1)}, u32[]{:S(2)}) copy-start(bf16[2,256,128]{2,1,0:T(8,128)(2,1)S(1)} %collective-permute-done.29.refs_6_) | copy-start | bytes 393220
  122.3 4.4 %copy-start.15 = (bf16[2,256,128]{2,1,0:T(8,128)(2,1)}, bf16[2,256,128]{2,1,0:T(8,128)(2,1)S(1)}, u32[]{:S(2)}) copy-start(bf16[2,256,128]{2,1,0:T(8,128)(2,1)S(1)} %collective-permute-done.30.refs_7_) | copy-start | bytes 393220
  122.4 4.4 %copy-start.16 = (bf16[2,256,128]{2,1,0:T(8,128)(2,1)}, bf16[2,256,128]{2,1,0:T(8,128)(2,1)S(1)}, u32[]{:S(2)}) copy-start(bf16[2,256,128]{2,1,0:T(8,128)(2,1)S(1)} %collective-permute-done.14.refs_1_) | copy-start | bytes 393220
  (9 other events, 13.0 us)
where the time goes:
time: 132 us; the launch traced here: 130 us
  starting transfers between devices  49.2 us (37%)
  Pallas kernels  39.9 us (30%)
  waiting for transfers between devices  33.5 us (25%)
  local copies, waits for them, and re-layouts  4.33 us (3%)
  other arithmetic  1.89 us (1%)
    ppermute x31, starting transfers between devices, send(): return lax.ppermute(array, 'seq', perm)  49.2 us
    ppermute x31, waiting for transfers between devices, send(): return lax.ppermute(array, 'seq', perm)  33.5 us
    pallas_call x4, Pallas kernels, attend(): pl.pallas_call(body, grid=(KH,), in_specs=in_specs, out_specs=out_specs,...  29.8 us
    pallas_call x2, Pallas kernels, pack_kv(): pl.pallas_call(body, grid=(1,), in_specs=[pl.BlockSpec(memory_space=pltpu...  3.66 us
    unnamed x52, local copies, waits for them, and re-layouts  2.88 us
  transfers between devices with their start and end apart: 31, of which 9 were waited for; matrix products, arithmetic and copies ran while one was open for 2% of the time, Pallas kernels for 27%

commit v1 on v0

--- a/solution.py
+++ b/solution.py
@@ -6,6 +6,7 @@
 from jax.experimental import pallas as pl
 from jax.experimental.pallas import tpu as pltpu
 from jax.sharding import PartitionSpec as P
+
 
 HQ = 64
 HK = 8
@@ -16,7 +17,9 @@
 QUAD = 4
 RING = 8
 KH = HK // QUAD
-PHASES = ((0, 7, 1, 6, 2), (5, 3, 4))
+PHASES = ((0, 7, 1), (6, 2), (5, 3), (4,))
+ATTEND_VMEM = 24 << 20
+SMALL_VMEM = 8 << 20
 SCALE = math.log2(math.e) / math.sqrt(DH)
 
 
@@ -32,8 +35,9 @@
     return (place_ref[0] // 16) * 2 + place_ref[0] % 2
 
 
-def pack_kv(s, place, cache_keys, cache_values, stretch_keys, stretch_values):
-    pre, new = cache_keys.shape[1], stretch_keys.shape[1]
+def pack_kv(place, cache_keys, cache_values, stretch_keys, stretch_values):
+    seqs, pre, _ = cache_keys.shape
+    new = stretch_keys.shape[1]
 
     def body(place_ref, ck, cv, sk, sv, *outs):
         own = corner(place_ref)
@@ -41,20 +45,19 @@
             for h in range(KH):
                 at = pl.ds(pl.multiple_of((own ^ r) * (KH * DH) + h * DH, DH), DH)
                 for kv, (old, fresh) in enumerate(((ck, sk), (cv, sv))):
-                    outs[r][kv, h, :pre, :] = old[0, :, at]
-                    outs[r][kv, h, pre:, :] = fresh[0, :, at]
-
-    shape = (2, KH, pre + new, DH)
-    spec = lambda x: pl.BlockSpec((1,) + x.shape[1:], lambda i: (s, 0, 0))
-    arrays = (cache_keys, cache_values, stretch_keys, stretch_values)
-    return pl.pallas_call(
-        body,
-        grid=(1,),
-        in_specs=[pl.BlockSpec(memory_space=pltpu.SMEM)] + [spec(x) for x in arrays],
-        out_specs=[pl.BlockSpec(shape, lambda i: (0, 0, 0, 0))] * QUAD,
-        out_shape=[jax.ShapeDtypeStruct(shape, jnp.bfloat16)] * QUAD,
+                    for s in range(seqs):
+                        outs[r][kv, s, h, :pre, :] = old[s, :, at]
+                        outs[r][kv, s, h, pre:, :] = fresh[s, :, at]
+
+    shape = jax.ShapeDtypeStruct((2, seqs, KH, pre + new, DH), jnp.bfloat16)
+    return pl.pallas_call(
+        body,
+        in_specs=[pl.BlockSpec(memory_space=pltpu.SMEM)] + [pl.BlockSpec(memory_space=pltpu.VMEM)] * 4,
+        out_specs=[pl.BlockSpec(memory_space=pltpu.VMEM)] * QUAD,
+        out_shape=[shape] * QUAD,
+        compiler_params=pltpu.CompilerParams(vmem_limit_bytes=SMALL_VMEM),
         name="pack_kv",
-    )(place, *arrays)
+    )(place, *[pltpu.with_memory_space_constraint(x, pltpu.HBM) for x in (cache_keys, cache_values, stretch_keys, stretch_values)])
 
 
 def pack_q(place, queries):
@@ -75,6 +78,7 @@
         in_specs=[pl.BlockSpec(memory_space=pltpu.SMEM), pl.BlockSpec((1, rows, HQ * DH), lambda s: (s, 0, 0))],
         out_specs=[pl.BlockSpec(block, lambda s: (s, 0, 0, 0))] * QUAD,
         out_shape=[jax.ShapeDtypeStruct((seqs,) + block[1:], jnp.bfloat16)] * QUAD,
+        compiler_params=pltpu.CompilerParams(vmem_limit_bytes=SMALL_VMEM),
         name="pack_q",
     )(place, queries)
 
@@ -98,6 +102,7 @@
         in_specs=[pl.BlockSpec(memory_space=pltpu.SMEM)] + [pl.BlockSpec(memory_space=pltpu.VMEM)] * (seqs * QUAD),
         out_specs=pl.BlockSpec(memory_space=pltpu.VMEM),
         out_shape=jax.ShapeDtypeStruct((seqs, rows, HQ * DH), jnp.bfloat16),
+        compiler_params=pltpu.CompilerParams(vmem_limit_bytes=SMALL_VMEM),
         name="unpack_out",
     )(place, *[p for one in pieces for p in one])
 
@@ -129,6 +134,7 @@
             jax.ShapeDtypeStruct((seqs, pre // PAGE, 2 * width), jnp.bfloat16),
             jax.ShapeDtypeStruct((seqs, new // PAGE, 2 * width), jnp.bfloat16),
         ],
+        compiler_params=pltpu.CompilerParams(vmem_limit_bytes=SMALL_VMEM),
         name="page_bounds",
     )(place, prefix_len, cache_keys, stretch_keys)
 
@@ -136,15 +142,14 @@
 def attend(s, place, prefix_len, queries, blocks, which, state, last, rows):
     count = len(blocks)
     tile = GROUP * rows
-    pre = blocks[0][0].shape[3] - rows
-    old_chunks = QUAD * pre // DH
-    chunks = old_chunks + QUAD * rows // DH
+    slots = QUAD // 2
+    pre = blocks[0][0].shape[4] - rows
+    half_rows = slots * rows
 
     def body(*refs):
         place_ref, len_ref = refs[:2]
         q_refs = refs[2 : 2 + QUAD]
-        k_refs = refs[2 + QUAD : 2 + QUAD + count]
-        v_refs = refs[2 + QUAD + count : 2 + QUAD + 2 * count]
+        half_refs = refs[2 + QUAD : 2 + QUAD + 2 * count]
         rest = refs[2 + QUAD + 2 * count : -1]
         score_ref = refs[-1]
         if state is not None:
@@ -164,32 +169,40 @@
                 pos = jnp.where(lane >= k * width, shard(first + k, d) * width + lane - k * width, pos)
             return pos
 
-        per = DH // pre
-        fade = [
-            [jnp.where(spread(c * per, pre, d) < len_ref[s], 0.0, NEG) for c in range(old_chunks)] for d in which
-        ]
-        new_pos = [spread(0, rows, d) for d in which]
-        ones = jnp.ones((QUAD * (pre + rows), DH), jnp.bfloat16)
-
-        def side(ref):
-            old = ref[0, :, 0, :pre, :].reshape(QUAD * pre, DH)
-            return jnp.concatenate([old, ref[0, :, 0, pre:, :].reshape(QUAD * rows, DH)], axis=0)
+        def old_part(ref, kv):
+            return ref[:, kv, 0, 0, :pre, :].reshape(slots * pre, DH)
+
+        def new_part(ref, kv):
+            return ref[:, kv, 0, 0, pre:, :].reshape(half_rows, DH)
+
+        chunks = []
+        for b, d in enumerate(which):
+            for half in range(2):
+                ref = half_refs[2 * b + half]
+                fade = jnp.where(spread(half * slots, pre, d) < len_ref[s], 0.0, NEG)
+                chunks.append((lambda kv, ref=ref: old_part(ref, kv), fade, None))
+        for b, d in enumerate(which):
+            low, high = half_refs[2 * b : 2 * b + 2]
+            both = lambda kv, low=low, high=high: jnp.concatenate([new_part(low, kv), new_part(high, kv)], axis=0)
+            chunks.append((both, None, spread(0, rows, d)))
+        groups = [chunks[i : i + 2] for i in range(0, len(chunks), 2)]
 
         def score(r):
             q = q_refs[r][0, 0]
             row_pos = shard(r, 0) * rows + lax.broadcasted_iota(jnp.int32, (tile, DH), 0) % rows
             top = None
-            for b in range(count):
+            for g, group in enumerate(groups):
+                keys = jnp.concatenate([c[0](0) for c in group], axis=0)
                 part = lax.dot_general(
-                    q, side(k_refs[b]), (((1,), (1,)), ((), ())), preferred_element_type=jnp.float32
+                    q, keys, (((1,), (1,)), ((), ())), preferred_element_type=jnp.float32
                 )
-                for c in range(chunks):
+                for c, (_, fade, pos) in enumerate(group):
                     piece = part[:, c * DH : (c + 1) * DH]
-                    if c < old_chunks:
-                        piece = piece + fade[b][c]
+                    if fade is not None:
+                        piece = piece + fade
                     else:
-                        piece = jnp.where(new_pos[b] <= row_pos, piece, NEG)
-                    score_ref[r % 2, b * chunks + c] = piece
+                        piece = jnp.where(pos <= row_pos, piece, NEG)
+                    score_ref[r % 2, 2 * g + c] = piece
                     top = piece if top is None else jnp.maximum(top, piece)
             return top
 
@@ -200,14 +213,15 @@
                 old_top = top_in[0, at, :]
                 top = jnp.maximum(top, old_top)
             mixed = None
-            for b in range(count):
+            for g, group in enumerate(groups):
                 weights = [
-                    jnp.exp2((score_ref[r % 2, b * chunks + c] - top) * SCALE).astype(jnp.bfloat16)
-                    for c in range(chunks)
+                    jnp.exp2((score_ref[r % 2, 2 * g + c] - top) * SCALE).astype(jnp.bfloat16)
+                    for c in range(len(group))
                 ]
+                values = jnp.concatenate([c[0](1) for c in group], axis=0)
                 part = jnp.dot(
                     jnp.concatenate(weights, axis=1),
-                    jnp.concatenate([side(v_refs[b]), ones], axis=1),
+                    jnp.concatenate([values, jnp.ones_like(values)], axis=1),
                     preferred_element_type=jnp.float32,
                 )
                 mixed = part if mixed is None else mixed + part
@@ -229,16 +243,15 @@
             mix(r, tops)
             tops = following
 
-    kv_shape = (1, QUAD, 1) + blocks[0][0].shape[3:]
-    kv_spec = lambda x, i: pl.BlockSpec(kv_shape, lambda h: (min(i, x.shape[0] - 1), 0, h, 0, 0))
+    half_shape = (slots, 2, 1, 1) + blocks[0][0].shape[4:]
     state_specs = [
         pl.BlockSpec((1, QUAD * tile, 2 * DH), lambda h: (h, 0, 0)),
         pl.BlockSpec((1, QUAD * tile, DH), lambda h: (h, 0, 0)),
     ]
     in_specs = [pl.BlockSpec(memory_space=pltpu.SMEM)] * 2
     in_specs += [pl.BlockSpec((1, 1, tile, DH), lambda h: (s, h, 0, 0))] * QUAD
-    in_specs += [kv_spec(k, 0) for k, _ in blocks] + [kv_spec(v, 1) for _, v in blocks]
-    operands = [place, prefix_len, *queries, *[k for k, _ in blocks], *[v for _, v in blocks]]
+    in_specs += [pl.BlockSpec(half_shape, lambda h: (0, 0, s, h, 0, 0))] * (2 * count)
+    operands = [place, prefix_len, *queries, *[half for block in blocks for half in block]]
     if state is not None:
         in_specs += state_specs
         operands += list(state)
@@ -248,15 +261,17 @@
     else:
         out_specs = state_specs
         out_shape = [jax.ShapeDtypeStruct((KH, QUAD * tile, w), jnp.float32) for w in (2 * DH, DH)]
-    pairs = KH * QUAD * tile * chunks * DH * count
+    wide = count * (QUAD * (pre + rows)) // DH
+    pairs = KH * QUAD * tile * wide * DH
     return pl.pallas_call(
         body,
         grid=(KH,),
         in_specs=in_specs,
         out_specs=out_specs,
         out_shape=out_shape,
-        scratch_shapes=[pltpu.VMEM((2, count * chunks, tile, DH), jnp.float32)],
+        scratch_shapes=[pltpu.VMEM((2, wide, tile, DH), jnp.float32)],
         cost_estimate=pl.CostEstimate(flops=4 * DH * pairs, transcendentals=pairs, bytes_accessed=4 << 20),
+        compiler_params=pltpu.CompilerParams(vmem_limit_bytes=ATTEND_VMEM),
         name="attend",
     )(*operands)
 
@@ -269,36 +284,29 @@
     seqs, rows, _ = queries.shape
     place = lax.axis_index("seq").astype(jnp.int32).reshape(1)
 
-    mine = []
-    for s in range(seqs):
-        pieces = pack_kv(s, place, cache_keys, cache_values, stretch_keys, stretch_values)
-        got = [pieces[0]] + [send(pieces[r], quad_perm(r)) for r in range(1, QUAD)]
-        mine.append(jnp.stack(got, axis=1))
+    pieces = pack_kv(place, cache_keys, cache_values, stretch_keys, stretch_values)
+    got = [pieces[0]] + [send(pieces[r], quad_perm(r)) for r in range(1, QUAD)]
     packed = pack_q(place, queries)
     q_tiles = [packed[0]] + [send(packed[r], quad_perm(r)) for r in range(1, QUAD)]
     prefix_bounds, stretch_bounds = bounds(place, prefix_len, cache_keys, stretch_keys)
 
-    blocks = [{0: (m, m)} for m in mine]
-    half = RING // 2
-    for step in range(1, half):
-        for s in range(seqs):
-            forth = send(blocks[s][(1 - step) % RING][0], ring_perm(1))
-            back = send(blocks[s][step - 1][0], ring_perm(-1))
-            blocks[s][-step % RING] = (forth, forth)
-            blocks[s][step] = (back, back)
-    for s in range(seqs):
-        forth = send(blocks[s][half + 1][0][:1], ring_perm(1))
-        back = send(blocks[s][half - 1][1][1:], ring_perm(-1))
-        blocks[s][half] = (forth, back)
+    rings = []
+    for n in range(2):
+        ring = {0: jnp.stack(got[2 * n : 2 * n + 2])}
+        for step in range(1, RING // 2 + 1):
+            if step < RING // 2 or n == 0:
+                ring[-step % RING] = send(ring[(1 - step) % RING], ring_perm(1))
+            if step < RING // 2 or n == 1:
+                ring[step] = send(ring[step - 1], ring_perm(-1))
+        rings.append(ring)
 
     sent = []
     for s in range(seqs):
         state = None
         for n, which in enumerate(PHASES):
             last = n + 1 == len(PHASES)
-            state = attend(
-                s, place, prefix_len, q_tiles, [blocks[s][d] for d in which], which, state, last, rows
-            )
+            blocks = [(rings[0][d], rings[1][d]) for d in which]
+            state = attend(s, place, prefix_len, q_tiles, blocks, which, state, last, rows)
         sent.append([state[0]] + [send(state[r], quad_perm(r)) for r in range(1, QUAD)])
     attention = unpack_out(place, sent, rows)
     return attention, prefix_bounds, stretch_bounds

time: 132 us -> 112 us (0.85)
  starting transfers between devices: 49.2 us -> 39.8 us
  Pallas kernels: 39.9 us -> 32.4 us
  local copies, waits for them, and re-layouts: 4.33 us -> 0.02 us
  waiting for transfers between devices: 33.5 us -> 37 us
  other arithmetic: 1.89 us -> 0.08 us
    ppermute x31 -> x26, starting transfers between devices: 49.2 us -> 39.8 us  [send(): return lax.ppermute(array, 'seq', perm)]
    ppermute x31 -> x26, waiting for transfers between devices: 33.5 us -> 37 us  [send(): return lax.ppermute(array, 'seq', perm)]
    unnamed x52 -> x8, local copies, waits for them, and re-layouts: 2.88 us -> 0.02 us
    pallas_call x2 -> x1, Pallas kernels: 3.66 us -> 1.39 us  [pack_kv(): pl.pallas_call(body, in_specs=[pl.BlockSpec(memory_space=pltpu.SMEM)] + [...]
    another operation x2, other arithmetic: 1.89 us -> 0.08 us  [run(): ring = {0: jnp.stack(got[2 * n:2 * n + 2])}]
    pallas_call x1, Pallas kernels: 2.14 us -> 0.34 us  [pack_q(): pl.pallas_call(body, grid=(seqs,), in_specs=[pl.BlockSpec(memory_space=pl...]
    pallas_call x4 -> x8, Pallas kernels: 29.8 us -> 28.1 us  [attend(): pl.pallas_call(body, grid=(KH,), in_specs=in_specs, out_specs=out_specs,...]
    slice x4 -> x0, local copies, waits for them, and re-layouts: 1.45 us -> none  [the longest x2 0.73 us: run(): back = send(blocks[s][half - 1][1][1:], ring_perm(-1))]
  transfers between devices with their start and end apart: 31 -> 26, of which waited for: 9 -> 11; matrix products, arithmetic and copies ran while one was open for 2% -> 0% of each run, Pallas kernels for 27% -> 25%
where the time goes in v1:
time: 112 us; the launch traced here: 110 us
  starting transfers between devices  39.8 us (36%)
  waiting for transfers between devices  37 us (33%)
  Pallas kernels  32.4 us (29%)
    ppermute x26, starting transfers between devices, send(): return lax.ppermute(array, 'seq', perm)  39.8 us
    ppermute x26, waiting for transfers between devices, send(): return lax.ppermute(array, 'seq', perm)  37 us
    pallas_call x8, Pallas kernels, attend(): pl.pallas_call(body, grid=(KH,), in_specs=in_specs, out_specs=out_specs,...  28.1 us
  transfers between devices with their start and end apart: 26, of which 11 were waited for; matrix products, arithmetic and copies ran while one was open for 0% of the time, Pallas kernels for 25%

profile of v1, /device:TPU:7, one launch (start us, length us, event | category | flops | bytes accessed | tf_op | source)
XLA Modules:
  0.0 110.1 jit_solution(6281520434325393825)
XLA Ops:
  0.7 1.4 %pack_kv.1 = (bf16[2,2,2,96,128]{4,3,2,1,0:T(8,128)(2,1)S(1)}, bf16[2,2,2,96,128]{4,3,2,1,0:T(8,128)(2,1)S(1)}, bf16[2,2,2,96,128]{4,3,2,1,0:T(8,128)(2,1)S(1)}, bf16[2,2,2,96,128]{4,3,2,1,0:T(8,128)(2,1)S(1)}) custom-call(s32[1]{0:T(128)} %bitcast.place_ref.refs_0_, bf16[2,64,1024]{2,1,0:T(8,128)(2,1)} %ck.3, bf16[2,64,1024]{2,1,0:T(8,128)(2,1)} %cv.1, ...), custom_call_target="tpu_custom_call" | custom-call | tf_op jit(solution)/shard_map/pack_kv/pallas_call | solution.py:53
  2.1 1.2 %collective-permute-start.8 = (bf16[2,2,2,96,128]{4,3,2,1,0:T(8,128)(2,1)S(1)}, bf16[2,2,2,96,128]{4,3,2,1,0:T(8,128)(2,1)S(1)}, u32[]{:S(2)}, u32[]{:S(2)}) collective-permute-start(bf16[2,2,2,96,128]{4,3,2,1,0:T(8,128)(2,1)S(1)} %get-tuple-element.39), channel_id=1, source_target_pairs={{0,16},{1,17},{2,18},{3,19},{4,20},{5,21},{6,22},{7,23},{8,24},{9,... | collective-permute-start | bytes 589832 | tf_op jit(solution)/shard_map/ppermute | solution.py:280
  3.3 2.7 %collective-permute-start.9 = (bf16[2,2,2,96,128]{4,3,2,1,0:T(8,128)(2,1)S(1)}, bf16[2,2,2,96,128]{4,3,2,1,0:T(8,128)(2,1)S(1)}, u32[]{:S(2)}, u32[]{:S(2)}) collective-permute-start(bf16[2,2,2,96,128]{4,3,2,1,0:T(8,128)(2,1)S(1)} %get-tuple-element.40), channel_id=1, source_target_pairs={{0,17},{1,16},{2,19},{3,18},{4,21},{5,20},{6,23},{7,22},{8,25},{9,... | collective-permute-start | bytes 589832 | tf_op jit(solution)/shard_map/ppermute | solution.py:280
  5.9 0.0 collective-permute-start.3
  6.0 3.5 %collective-permute-done.8 = bf16[2,2,2,96,128]{4,3,2,1,0:T(8,128)(2,1)S(1)} collective-permute-done((bf16[2,2,2,96,128]{4,3,2,1,0:T(8,128)(2,1)S(1)}, bf16[2,2,2,96,128]{4,3,2,1,0:T(8,128)(2,1)S(1)}, u32[]{:S(2)}, u32[]{:S(2)}) %collective-permute-start.8) | collective-permute-done | bytes 196640 | tf_op jit(solution)/shard_map/ppermute | solution.py:280
  9.4 5.1 %collective-permute-done.9 = bf16[2,2,2,96,128]{4,3,2,1,0:T(8,128)(2,1)S(1)} collective-permute-done((bf16[2,2,2,96,128]{4,3,2,1,0:T(8,128)(2,1)S(1)}, bf16[2,2,2,96,128]{4,3,2,1,0:T(8,128)(2,1)S(1)}, u32[]{:S(2)}, u32[]{:S(2)}) %collective-permute-start.9) | collective-permute-done | bytes 196640 | tf_op jit(solution)/shard_map/ppermute | solution.py:280
  14.5 5.7 %collective-permute-start.10 = (bf16[2,2,2,2,96,128]{5,4,3,2,1,0:T(8,128)(2,1)S(1)}, bf16[2,2,2,2,96,128]{5,4,3,2,1,0:T(8,128)(2,1)S(1)}, u32[]{:S(2)}, u32[]{:S(2)}) collective-permute-start(bf16[2,2,2,2,96,128]{5,4,3,2,1,0:T(8,128)(2,1)S(1)} %pad_maximum_fusion.1.refs_7_), channel_id=1, source_target_pairs={{0,14},{1,15},{2,0},{3,1},{4,2},{5,3},{6,4},{7,5},{8,6},{9,7},{10,... | collective-permute-start | bytes 1179656 | tf_op jit(solution)/shard_map/ppermute | solution.py:280
  20.2 0.0 collective-permute-done.3
  20.2 0.1 collective-permute-start.4
  20.3 0.1 collective-permute-start.14
  20.4 2.7 %collective-permute-start.17 = (bf16[2,2,2,2,96,128]{5,4,3,2,1,0:T(8,128)(2,1)S(1)}, bf16[2,2,2,2,96,128]{5,4,3,2,1,0:T(8,128)(2,1)S(1)}, u32[]{:S(2)}, u32[]{:S(2)}) collective-permute-start(bf16[2,2,2,2,96,128]{5,4,3,2,1,0:T(8,128)(2,1)S(1)} %pad_maximum_fusion.refs_6_), channel_id=1, source_target_pairs={{0,14},{1,15},{2,0},{3,1},{4,2},{5,3},{6,4},{7,5},{8,6},{9,7},{10,... | collective-permute-start | bytes 1179656 | tf_op jit(solution)/shard_map/ppermute | solution.py:280
  23.1 6.0 %collective-permute-done.10.refs_11_ = bf16[2,2,2,2,96,128]{5,4,3,2,1,0:T(8,128)(2,1)S(1)} collective-permute-done((bf16[2,2,2,2,96,128]{5,4,3,2,1,0:T(8,128)(2,1)S(1)}, bf16[2,2,2,2,96,128]{5,4,3,2,1,0:T(8,128)(2,1)S(1)}, u32[]{:S(2)}, u32[]{:S(2)}) %collective-permute-start.10) | collective-permute-done | bytes 393248 | tf_op jit(solution)/shard_map/ppermute | solution.py:280
  29.1 3.4 %collective-permute-start.11 = (bf16[2,2,2,2,96,128]{5,4,3,2,1,0:T(8,128)(2,1)S(1)}, bf16[2,2,2,2,96,128]{5,4,3,2,1,0:T(8,128)(2,1)S(1)}, u32[]{:S(2)}, u32[]{:S(2)}) collective-permute-start(bf16[2,2,2,2,96,128]{5,4,3,2,1,0:T(8,128)(2,1)S(1)} %collective-permute-done.10.refs_11_), channel_id=1, source_target_pairs={{0,14},{1,15},{2,0},{3,1},{4,2},{5,3},{6,4},{7,5},{8,6},{9,7},{10,... | collective-permute-start | bytes 1179656 | tf_op jit(solution)/shard_map/ppermute | solution.py:280
  32.5 0.0 collective-permute-done.4.refs_8_
  32.5 0.0 collective-permute-start.5
  32.5 0.3 pack_q.1
  32.9 0.9 collective-permute-start
  33.7 1.2 %collective-permute-done.refs_3_ = bf16[2,2,256,128]{3,2,1,0:T(8,128)(2,1)S(1)} collective-permute-done((bf16[2,2,256,128]{3,2,1,0:T(8,128)(2,1)S(1)}, bf16[2,2,256,128]{3,2,1,0:T(8,128)(2,1)S(1)}, u32[]{:S(2)}, u32[]{:S(2)}) %collective-permute-start) | collective-permute-done | bytes 262176 | tf_op jit(solution)/shard_map/ppermute | solution.py:280
  34.9 1.1 %collective-permute-start.1 = (bf16[2,2,256,128]{3,2,1,0:T(8,128)(2,1)S(1)}, bf16[2,2,256,128]{3,2,1,0:T(8,128)(2,1)S(1)}, u32[]{:S(2)}, u32[]{:S(2)}) collective-permute-start(bf16[2,2,256,128]{3,2,1,0:T(8,128)(2,1)S(1)} %get-tuple-element.35), channel_id=1, source_target_pairs={{0,16},{1,17},{2,18},{3,19},{4,20},{5,21},{6,22},{7,23},{8,24},{9,... | collective-permute-start | bytes 786440 | tf_op jit(solution)/shard_map/ppermute | solution.py:280
  36.0 4.7 %collective-permute-done.14.refs_9_ = bf16[2,2,2,2,96,128]{5,4,3,2,1,0:T(8,128)(2,1)S(1)} collective-permute-done((bf16[2,2,2,2,96,128]{5,4,3,2,1,0:T(8,128)(2,1)S(1)}, bf16[2,2,2,2,96,128]{5,4,3,2,1,0:T(8,128)(2,1)S(1)}, u32[]{:S(2)}, u32[]{:S(2)}) %collective-permute-start.14) | collective-permute-done | bytes 393248 | tf_op jit(solution)/shard_map/ppermute | solution.py:280
  40.8 2.7 %collective-permute-start.18 = (bf16[2,2,2,2,96,128]{5,4,3,2,1,0:T(8,128)(2,1)S(1)}, bf16[2,2,2,2,96,128]{5,4,3,2,1,0:T(8,128)(2,1)S(1)}, u32[]{:S(2)}, u32[]{:S(2)}) collective-permute-start(bf16[2,2,2,2,96,128]{5,4,3,2,1,0:T(8,128)(2,1)S(1)} %collective-permute-done.17.refs_10_), channel_id=1, source_target_pairs={{0,14},{1,15},{2,0},{3,1},{4,2},{5,3},{6,4},{7,5},{8,6},{9,7},{10,... | collective-permute-start | bytes 1179656 | tf_op jit(solution)/shard_map/ppermute | solution.py:280
  43.5 2.5 %collective-permute-done.11.refs_9_ = bf16[2,2,2,2,96,128]{5,4,3,2,1,0:T(8,128)(2,1)S(1)} collective-permute-done((bf16[2,2,2,2,96,128]{5,4,3,2,1,0:T(8,128)(2,1)S(1)}, bf16[2,2,2,2,96,128]{5,4,3,2,1,0:T(8,128)(2,1)S(1)}, u32[]{:S(2)}, u32[]{:S(2)}) %collective-permute-start.11) | collective-permute-done | bytes 393248 | tf_op jit(solution)/shard_map/ppermute | solution.py:280
  45.9 3.4 %collective-permute-start.12 = (bf16[2,2,2,2,96,128]{5,4,3,2,1,0:T(8,128)(2,1)S(1)}, bf16[2,2,2,2,96,128]{5,4,3,2,1,0:T(8,128)(2,1)S(1)}, u32[]{:S(2)}, u32[]{:S(2)}) collective-permute-start(bf16[2,2,2,2,96,128]{5,4,3,2,1,0:T(8,128)(2,1)S(1)} %collective-permute-done.11.refs_9_), channel_id=1, source_target_pairs={{0,14},{1,15},{2,0},{3,1},{4,2},{5,3},{6,4},{7,5},{8,6},{9,7},{10,... | collective-permute-start | bytes 1179656 | tf_op jit(solution)/shard_map/ppermute | solution.py:280
  49.4 1.9 %collective-permute-start.2 = (bf16[2,2,256,128]{3,2,1,0:T(8,128)(2,1)S(1)}, bf16[2,2,256,128]{3,2,1,0:T(8,128)(2,1)S(1)}, u32[]{:S(2)}, u32[]{:S(2)}) collective-permute-start(bf16[2,2,256,128]{3,2,1,0:T(8,128)(2,1)S(1)} %get-tuple-element.36), channel_id=1, source_target_pairs={{0,17},{1,16},{2,19},{3,18},{4,21},{5,20},{6,23},{7,22},{8,25},{9,... | collective-permute-start | bytes 786440 | tf_op jit(solution)/shard_map/ppermute | solution.py:280
  51.2 6.4 %collective-permute-done.15.refs_7_ = bf16[2,2,2,2,96,128]{5,4,3,2,1,0:T(8,128)(2,1)S(1)} collective-permute-done((bf16[2,2,2,2,96,128]{5,4,3,2,1,0:T(8,128)(2,1)S(1)}, bf16[2,2,2,2,96,128]{5,4,3,2,1,0:T(8,128)(2,1)S(1)}, u32[]{:S(2)}, u32[]{:S(2)}) %collective-permute-start.15) | collective-permute-done | bytes 393248 | tf_op jit(solution)/shard_map/ppermute | solution.py:280
  57.6 0.0 collective-permute-start.16
  57.6 2.7 %collective-permute-start.19 = (bf16[2,2,2,2,96,128]{5,4,3,2,1,0:T(8,128)(2,1)S(1)}, bf16[2,2,2,2,96,128]{5,4,3,2,1,0:T(8,128)(2,1)S(1)}, u32[]{:S(2)}, u32[]{:S(2)}) collective-permute-start(bf16[2,2,2,2,96,128]{5,4,3,2,1,0:T(8,128)(2,1)S(1)} %collective-permute-done.18.refs_8_), channel_id=1, source_target_pairs={{0,14},{1,15},{2,0},{3,1},{4,2},{5,3},{6,4},{7,5},{8,6},{9,7},{10,... | collective-permute-start | bytes 1179656 | tf_op jit(solution)/shard_map/ppermute | solution.py:280
  60.3 2.5 %collective-permute-done.12.refs_9_ = bf16[2,2,2,2,96,128]{5,4,3,2,1,0:T(8,128)(2,1)S(1)} collective-permute-done((bf16[2,2,2,2,96,128]{5,4,3,2,1,0:T(8,128)(2,1)S(1)}, bf16[2,2,2,2,96,128]{5,4,3,2,1,0:T(8,128)(2,1)S(1)}, u32[]{:S(2)}, u32[]{:S(2)}) %collective-permute-start.12) | collective-permute-done | bytes 393248 | tf_op jit(solution)/shard_map/ppermute | solution.py:280
  62.8 3.4 %collective-permute-start.13 = (bf16[2,2,2,2,96,128]{5,4,3,2,1,0:T(8,128)(2,1)S(1)}, bf16[2,2,2,2,96,128]{5,4,3,2,1,0:T(8,128)(2,1)S(1)}, u32[]{:S(2)}, u32[]{:S(2)}) collective-permute-start(bf16[2,2,2,2,96,128]{5,4,3,2,1,0:T(8,128)(2,1)S(1)} %collective-permute-done.12.refs_9_), channel_id=1, source_target_pairs={{0,14},{1,15},{2,0},{3,1},{4,2},{5,3},{6,4},{7,5},{8,6},{9,7},{10,... | collective-permute-start | bytes 1179656 | tf_op jit(solution)/shard_map/ppermute | solution.py:280
  66.2 4.7 %attend.12 = (f32[2,1024,256]{2,1,0:T(8,128)S(1)}, f32[2,1024,128]{2,1,0:T(8,128)S(1)}) custom-call(s32[1]{0:T(128)} %bitcast.place_ref.refs_0_, s32[2]{0:T(128)S(1)} %copy-done.3, bf16[2,2,256,128]{3,2,1,0:T(8,128)(2,1)S(1)} %get-tuple-element.33.refs_2_, bf16[2,2,256,128]{3,2,1,0:T(8,128)(2,1)S(1)} %collective-permute-done.refs_3_, ...), custom_call_target="tpu_custom_call" | custom-call | flops 1207959552 | bytes 4194304 | tf_op jit(solution)/shard_map/attend/pallas_call | solution.py:266
  71.0 4.7 %attend.8 = (f32[2,1024,256]{2,1,0:T(8,128)S(1)}, f32[2,1024,128]{2,1,0:T(8,128)S(1)}) custom-call(s32[1]{0:T(128)} %bitcast.place_ref.refs_0_, s32[2]{0:T(128)S(1)} %copy-done.3, bf16[2,2,256,128]{3,2,1,0:T(8,128)(2,1)S(1)} %get-tuple-element.33.refs_2_, bf16[2,2,256,128]{3,2,1,0:T(8,128)(2,1)S(1)} %collective-permute-done.refs_3_, ...), custom_call_target="tpu_custom_call" | custom-call | flops 1207959552 | bytes 4194304 | tf_op jit(solution)/shard_map/attend/pallas_call | solution.py:266
  75.7 3.3 %attend.13 = (f32[2,1024,256]{2,1,0:T(8,128)S(1)}, f32[2,1024,128]{2,1,0:T(8,128)S(1)}) custom-call(s32[1]{0:T(128)} %bitcast.place_ref.refs_0_, s32[2]{0:T(128)S(1)} %copy-done.3, bf16[2,2,256,128]{3,2,1,0:T(8,128)(2,1)S(1)} %get-tuple-element.33.refs_2_, bf16[2,2,256,128]{3,2,1,0:T(8,128)(2,1)S(1)} %collective-permute-done.refs_3_, ...), custom_call_target="tpu_custom_call" | custom-call | flops 805306368 | bytes 4194304 | tf_op jit(solution)/shard_map/attend/pallas_call | solution.py:266
  79.1 3.3 %attend.14 = (f32[2,1024,256]{2,1,0:T(8,128)S(1)}, f32[2,1024,128]{2,1,0:T(8,128)S(1)}) custom-call(s32[1]{0:T(128)} %bitcast.place_ref.refs_0_, s32[2]{0:T(128)S(1)} %copy-done.3, bf16[2,2,256,128]{3,2,1,0:T(8,128)(2,1)S(1)} %get-tuple-element.33.refs_2_, bf16[2,2,256,128]{3,2,1,0:T(8,128)(2,1)S(1)} %collective-permute-done.refs_3_, ...), custom_call_target="tpu_custom_call" | custom-call | flops 805306368 | bytes 4194304 | tf_op jit(solution)/shard_map/attend/pallas_call | solution.py:266
  82.4 0.5 collective-permute-done.7.refs_6_
  82.9 2.6 %attend.15 = (bf16[2,256,128]{2,1,0:T(8,128)(2,1)S(1)}, bf16[2,256,128]{2,1,0:T(8,128)(2,1)S(1)}, bf16[2,256,128]{2,1,0:T(8,128)(2,1)S(1)}, bf16[2,256,128]{2,1,0:T(8,128)(2,1)S(1)}) custom-call(s32[1]{0:T(128)} %bitcast.place_ref.refs_0_, s32[2]{0:T(128)S(1)} %copy-done.3, bf16[2,2,256,128]{3,2,1,0:T(8,128)(2,1)S(1)} %get-tuple-element.33.refs_2_, ...), custom_call_target="tpu_custom_call" | custom-call | flops 402653184 | bytes 4194304 | tf_op jit(solution)/shard_map/attend/pallas_call | solution.py:266
  85.6 1.0 collective-permute-start.23
  86.6 3.3 %attend.9 = (f32[2,1024,256]{2,1,0:T(8,128)S(1)}, f32[2,1024,128]{2,1,0:T(8,128)S(1)}) custom-call(s32[1]{0:T(128)} %bitcast.place_ref.refs_0_, s32[2]{0:T(128)S(1)} %copy-done.3, bf16[2,2,256,128]{3,2,1,0:T(8,128)(2,1)S(1)} %get-tuple-element.33.refs_2_, bf16[2,2,256,128]{3,2,1,0:T(8,128)(2,1)S(1)} %collective-permute-done.refs_3_, ...), custom_call_target="tpu_custom_call" | custom-call | flops 805306368 | bytes 4194304 | tf_op jit(solution)/shard_map/attend/pallas_call | solution.py:266
  89.9 3.3 %attend.10 = (f32[2,1024,256]{2,1,0:T(8,128)S(1)}, f32[2,1024,128]{2,1,0:T(8,128)S(1)}) custom-call(s32[1]{0:T(128)} %bitcast.place_ref.refs_0_, s32[2]{0:T(128)S(1)} %copy-done.3, bf16[2,2,256,128]{3,2,1,0:T(8,128)(2,1)S(1)} %get-tuple-element.33.refs_2_, bf16[2,2,256,128]{3,2,1,0:T(8,128)(2,1)S(1)} %collective-permute-done.refs_3_, ...), custom_call_target="tpu_custom_call" | custom-call | flops 805306368 | bytes 4194304 | tf_op jit(solution)/shard_map/attend/pallas_call | solution.py:266
  93.2 1.2 %collective-permute-start.24 = (bf16[2,256,128]{2,1,0:T(8,128)(2,1)S(1)}, bf16[2,256,128]{2,1,0:T(8,128)(2,1)S(1)}, u32[]{:S(2)}, u32[]{:S(2)}) collective-permute-start(bf16[2,256,128]{2,1,0:T(8,128)(2,1)S(1)} %get-tuple-element.59), channel_id=1, source_target_pairs={{0,16},{1,17},{2,18},{3,19},{4,20},{5,21},{6,22},{7,23},{8,24},{9,... | collective-permute-start | bytes 393224 | tf_op jit(solution)/shard_map/ppermute | solution.py:280
  94.4 2.1 %collective-permute-start.25 = (bf16[2,256,128]{2,1,0:T(8,128)(2,1)S(1)}, bf16[2,256,128]{2,1,0:T(8,128)(2,1)S(1)}, u32[]{:S(2)}, u32[]{:S(2)}) collective-permute-start(bf16[2,256,128]{2,1,0:T(8,128)(2,1)S(1)} %get-tuple-element.60), channel_id=1, source_target_pairs={{0,17},{1,16},{2,19},{3,18},{4,21},{5,20},{6,23},{7,22},{8,25},{9,... | collective-permute-start | bytes 393224 | tf_op jit(solution)/shard_map/ppermute | solution.py:280
  96.5 2.6 %attend.11 = (bf16[2,256,128]{2,1,0:T(8,128)(2,1)S(1)}, bf16[2,256,128]{2,1,0:T(8,128)(2,1)S(1)}, bf16[2,256,128]{2,1,0:T(8,128)(2,1)S(1)}, bf16[2,256,128]{2,1,0:T(8,128)(2,1)S(1)}) custom-call(s32[1]{0:T(128)} %bitcast.place_ref.refs_0_, s32[2]{0:T(128)S(1)} %copy-done.3, bf16[2,2,256,128]{3,2,1,0:T(8,128)(2,1)S(1)} %get-tuple-element.33.refs_2_, ...), custom_call_target="tpu_custom_call" | custom-call | flops 402653184 | bytes 4194304 | tf_op jit(solution)/shard_map/attend/pallas_call | solution.py:266
  99.1 0.3 collective-permute-start.20
  99.4 1.1 %collective-permute-start.21 = (bf16[2,256,128]{2,1,0:T(8,128)(2,1)S(1)}, bf16[2,256,128]{2,1,0:T(8,128)(2,1)S(1)}, u32[]{:S(2)}, u32[]{:S(2)}) collective-permute-start(bf16[2,256,128]{2,1,0:T(8,128)(2,1)S(1)} %get-tuple-element.49), channel_id=1, source_target_pairs={{0,16},{1,17},{2,18},{3,19},{4,20},{5,21},{6,22},{7,23},{8,24},{9,... | collective-permute-start | bytes 393224 | tf_op jit(solution)/shard_map/ppermute | solution.py:280
  100.5 2.3 %collective-permute-start.22 = (bf16[2,256,128]{2,1,0:T(8,128)(2,1)S(1)}, bf16[2,256,128]{2,1,0:T(8,128)(2,1)S(1)}, u32[]{:S(2)}, u32[]{:S(2)}) collective-permute-start(bf16[2,256,128]{2,1,0:T(8,128)(2,1)S(1)} %get-tuple-element.50), channel_id=1, source_target_pairs={{0,17},{1,16},{2,19},{3,18},{4,21},{5,20},{6,23},{7,22},{8,25},{9,... | collective-permute-start | bytes 393224 | tf_op jit(solution)/shard_map/ppermute | solution.py:280
  102.9 1.4 %page_bounds.1 = (bf16[2,4,2048]{2,1,0:T(4,128)(2,1)}, bf16[2,2,2048]{2,1,0:T(2,128)(2,1)}) custom-call(s32[1]{0:T(128)} %bitcast.place_ref.refs_0_, s32[2]{0:T(128)S(1)} %copy-done.3, bf16[2,64,1024]{2,1,0:T(8,128)(2,1)S(1)} %copy-done.1, bf16[2,32,1024]{2,1,0:T(8,128)(2,1)S(1)} %copy-done.2), custom_call_target="tpu_custom_call" | custom-call | tf_op jit(solution)/shard_map/page_bounds/pallas_call | solution.py:129
  104.3 1.3 %collective-permute-done.21.refs_2_ = bf16[2,256,128]{2,1,0:T(8,128)(2,1)S(1)} collective-permute-done((bf16[2,256,128]{2,1,0:T(8,128)(2,1)S(1)}, bf16[2,256,128]{2,1,0:T(8,128)(2,1)S(1)}, u32[]{:S(2)}, u32[]{:S(2)}) %collective-permute-start.21) | collective-permute-done | bytes 131104 | tf_op jit(solution)/shard_map/ppermute | solution.py:280
  105.6 3.3 %collective-permute-done.22.refs_3_ = bf16[2,256,128]{2,1,0:T(8,128)(2,1)S(1)} collective-permute-done((bf16[2,256,128]{2,1,0:T(8,128)(2,1)S(1)}, bf16[2,256,128]{2,1,0:T(8,128)(2,1)S(1)}, u32[]{:S(2)}, u32[]{:S(2)}) %collective-permute-start.22) | collective-permute-done | bytes 131104 | tf_op jit(solution)/shard_map/ppermute | solution.py:280
  108.9 1.2 %unpack_out.1 = bf16[2,32,8192]{2,1,0:T(8,128)(2,1)} custom-call(s32[1]{0:T(128)} %bitcast.place_ref.refs_0_, bf16[2,256,128]{2,1,0:T(8,128)(2,1)S(1)} %get-tuple-element.47.refs_0_, bf16[2,256,128]{2,1,0:T(8,128)(2,1)S(1)} %collective-permute-done.20.refs_1_, bf16[2,256,128]{2,1,0:T(8,128)(2,1)S(1)} %collective-permute-done.21.refs_2_, ...), custom_call_target="tpu_custom_call" | custom-call | tf_op jit(solution)/shard_map/unpack_out/pallas_call | solution.py:100
  (26 shorter events, 0.1 us)
Async XLA Ops:
  0.6 31.9 %copy-start = (bf16[2,32,8192]{2,1,0:T(8,128)(2,1)S(1)}, bf16[2,32,8192]{2,1,0:T(8,128)(2,1)}, u32[]{:S(2)}) copy-start(bf16[2,32,8192]{2,1,0:T(8,128)(2,1)} %q.1) | copy-start | bytes 3145732
  0.6 65.6 %copy-start.3 = (s32[2]{0:T(128)S(1)}, s32[2]{0:T(128)}, u32[]{:S(2)}) copy-start(s32[2]{0:T(128)} %len_ref.1) | copy-start | bytes 28
  2.1 7.4 %collective-permute-start.8 = (bf16[2,2,2,96,128]{4,3,2,1,0:T(8,128)(2,1)S(1)}, bf16[2,2,2,96,128]{4,3,2,1,0:T(8,128)(2,1)S(1)}, u32[]{:S(2)}, u32[]{:S(2)}) collective-permute-start(bf16[2,2,2,96,128]{4,3,2,1,0:T(8,128)(2,1)S(1)} %get-tuple-element.39), channel_id=1, source_target_pairs={{0,16},{1,17},{2,18},{3,19},{4,20},{5,21},{6,22},{7,23},{8,24},{9,... | collective-permute-start | bytes 589832 | tf_op jit(solution)/shard_map/ppermute | solution.py:280
  3.3 11.2 %collective-permute-start.9 = (bf16[2,2,2,96,128]{4,3,2,1,0:T(8,128)(2,1)S(1)}, bf16[2,2,2,96,128]{4,3,2,1,0:T(8,128)(2,1)S(1)}, u32[]{:S(2)}, u32[]{:S(2)}) collective-permute-start(bf16[2,2,2,96,128]{4,3,2,1,0:T(8,128)(2,1)S(1)} %get-tuple-element.40), channel_id=1, source_target_pairs={{0,17},{1,16},{2,19},{3,18},{4,21},{5,20},{6,23},{7,22},{8,25},{9,... | collective-permute-start | bytes 589832 | tf_op jit(solution)/shard_map/ppermute | solution.py:280
  5.9 14.2 %collective-permute-start.3 = (bf16[2,2,2,96,128]{4,3,2,1,0:T(8,128)(2,1)S(1)}, bf16[2,2,2,96,128]{4,3,2,1,0:T(8,128)(2,1)S(1)}, u32[]{:S(2)}, u32[]{:S(2)}) collective-permute-start(bf16[2,2,2,96,128]{4,3,2,1,0:T(8,128)(2,1)S(1)} %get-tuple-element.38), channel_id=1, source_target_pairs={{0,1},{1,0},{2,3},{3,2},{4,5},{5,4},{6,7},{7,6},{8,9},{9,8},{10,11... | collective-permute-start | bytes 589832 | tf_op jit(solution)/shard_map/ppermute | solution.py:280
  14.5 14.6 %collective-permute-start.10 = (bf16[2,2,2,2,96,128]{5,4,3,2,1,0:T(8,128)(2,1)S(1)}, bf16[2,2,2,2,96,128]{5,4,3,2,1,0:T(8,128)(2,1)S(1)}, u32[]{:S(2)}, u32[]{:S(2)}) collective-permute-start(bf16[2,2,2,2,96,128]{5,4,3,2,1,0:T(8,128)(2,1)S(1)} %pad_maximum_fusion.1.refs_7_), channel_id=1, source_target_pairs={{0,14},{1,15},{2,0},{3,1},{4,2},{5,3},{6,4},{7,5},{8,6},{9,7},{10,... | collective-permute-start | bytes 1179656 | tf_op jit(solution)/shard_map/ppermute | solution.py:280
  20.2 12.3 %collective-permute-start.4 = (bf16[2,2,2,2,96,128]{5,4,3,2,1,0:T(8,128)(2,1)S(1)}, bf16[2,2,2,2,96,128]{5,4,3,2,1,0:T(8,128)(2,1)S(1)}, u32[]{:S(2)}, u32[]{:S(2)}) collective-permute-start(bf16[2,2,2,2,96,128]{5,4,3,2,1,0:T(8,128)(2,1)S(1)} %pad_maximum_fusion.refs_6_), channel_id=1, source_target_pairs={{0,2},{1,3},{2,4},{3,5},{4,6},{5,7},{6,8},{7,9},{8,10},{9,11},{10,... | collective-permute-start | bytes 1179656 | tf_op jit(solution)/shard_map/ppermute | solution.py:280
  20.3 20.5 %collective-permute-start.14 = (bf16[2,2,2,2,96,128]{5,4,3,2,1,0:T(8,128)(2,1)S(1)}, bf16[2,2,2,2,96,128]{5,4,3,2,1,0:T(8,128)(2,1)S(1)}, u32[]{:S(2)}, u32[]{:S(2)}) collective-permute-start(bf16[2,2,2,2,96,128]{5,4,3,2,1,0:T(8,128)(2,1)S(1)} %pad_maximum_fusion.1.refs_7_), channel_id=1, source_target_pairs={{0,2},{1,3},{2,4},{3,5},{4,6},{5,7},{6,8},{7,9},{8,10},{9,11},{10,... | collective-permute-start | bytes 1179656 | tf_op jit(solution)/shard_map/ppermute | solution.py:280
  20.4 20.4 %collective-permute-start.17 = (bf16[2,2,2,2,96,128]{5,4,3,2,1,0:T(8,128)(2,1)S(1)}, bf16[2,2,2,2,96,128]{5,4,3,2,1,0:T(8,128)(2,1)S(1)}, u32[]{:S(2)}, u32[]{:S(2)}) collective-permute-start(bf16[2,2,2,2,96,128]{5,4,3,2,1,0:T(8,128)(2,1)S(1)} %pad_maximum_fusion.refs_6_), channel_id=1, source_target_pairs={{0,14},{1,15},{2,0},{3,1},{4,2},{5,3},{6,4},{7,5},{8,6},{9,7},{10,... | collective-permute-start | bytes 1179656 | tf_op jit(solution)/shard_map/ppermute | solution.py:280
  29.1 16.9 %collective-permute-start.11 = (bf16[2,2,2,2,96,128]{5,4,3,2,1,0:T(8,128)(2,1)S(1)}, bf16[2,2,2,2,96,128]{5,4,3,2,1,0:T(8,128)(2,1)S(1)}, u32[]{:S(2)}, u32[]{:S(2)}) collective-permute-start(bf16[2,2,2,2,96,128]{5,4,3,2,1,0:T(8,128)(2,1)S(1)} %collective-permute-done.10.refs_11_), channel_id=1, source_target_pairs={{0,14},{1,15},{2,0},{3,1},{4,2},{5,3},{6,4},{7,5},{8,6},{9,7},{10,... | collective-permute-start | bytes 1179656 | tf_op jit(solution)/shard_map/ppermute | solution.py:280
  32.5 16.9 %collective-permute-start.5 = (bf16[2,2,2,2,96,128]{5,4,3,2,1,0:T(8,128)(2,1)S(1)}, bf16[2,2,2,2,96,128]{5,4,3,2,1,0:T(8,128)(2,1)S(1)}, u32[]{:S(2)}, u32[]{:S(2)}) collective-permute-start(bf16[2,2,2,2,96,128]{5,4,3,2,1,0:T(8,128)(2,1)S(1)} %collective-permute-done.4.refs_8_), channel_id=1, source_target_pairs={{0,2},{1,3},{2,4},{3,5},{4,6},{5,7},{6,8},{7,9},{8,10},{9,11},{10,... | collective-permute-start | bytes 1179656 | tf_op jit(solution)/shard_map/ppermute | solution.py:280
  32.9 2.0 %collective-permute-start = (bf16[2,2,256,128]{3,2,1,0:T(8,128)(2,1)S(1)}, bf16[2,2,256,128]{3,2,1,0:T(8,128)(2,1)S(1)}, u32[]{:S(2)}, u32[]{:S(2)}) collective-permute-start(bf16[2,2,256,128]{3,2,1,0:T(8,128)(2,1)S(1)} %get-tuple-element.34), channel_id=1, source_target_pairs={{0,1},{1,0},{2,3},{3,2},{4,5},{5,4},{6,7},{7,6},{8,9},{9,8},{10,11... | collective-permute-start | bytes 786440 | tf_op jit(solution)/shard_map/ppermute | solution.py:280
  34.9 14.5 %collective-permute-start.1 = (bf16[2,2,256,128]{3,2,1,0:T(8,128)(2,1)S(1)}, bf16[2,2,256,128]{3,2,1,0:T(8,128)(2,1)S(1)}, u32[]{:S(2)}, u32[]{:S(2)}) collective-permute-start(bf16[2,2,256,128]{3,2,1,0:T(8,128)(2,1)S(1)} %get-tuple-element.35), channel_id=1, source_target_pairs={{0,16},{1,17},{2,18},{3,19},{4,20},{5,21},{6,22},{7,23},{8,24},{9,... | collective-permute-start | bytes 786440 | tf_op jit(solution)/shard_map/ppermute | solution.py:280
  40.8 16.9 %collective-permute-start.15 = (bf16[2,2,2,2,96,128]{5,4,3,2,1,0:T(8,128)(2,1)S(1)}, bf16[2,2,2,2,96,128]{5,4,3,2,1,0:T(8,128)(2,1)S(1)}, u32[]{:S(2)}, u32[]{:S(2)}) collective-permute-start(bf16[2,2,2,2,96,128]{5,4,3,2,1,0:T(8,128)(2,1)S(1)} %collective-permute-done.14.refs_9_), channel_id=1, source_target_pairs={{0,2},{1,3},{2,4},{3,5},{4,6},{5,7},{6,8},{7,9},{8,10},{9,11},{10,... | collective-permute-start | bytes 1179656 | tf_op jit(solution)/shard_map/ppermute | solution.py:280
  40.8 16.9 %collective-permute-start.18 = (bf16[2,2,2,2,96,128]{5,4,3,2,1,0:T(8,128)(2,1)S(1)}, bf16[2,2,2,2,96,128]{5,4,3,2,1,0:T(8,128)(2,1)S(1)}, u32[]{:S(2)}, u32[]{:S(2)}) collective-permute-start(bf16[2,2,2,2,96,128]{5,4,3,2,1,0:T(8,128)(2,1)S(1)} %collective-permute-done.17.refs_10_), channel_id=1, source_target_pairs={{0,14},{1,15},{2,0},{3,1},{4,2},{5,3},{6,4},{7,5},{8,6},{9,7},{10,... | collective-permute-start | bytes 1179656 | tf_op jit(solution)/shard_map/ppermute | solution.py:280
  45.9 16.9 %collective-permute-start.12 = (bf16[2,2,2,2,96,128]{5,4,3,2,1,0:T(8,128)(2,1)S(1)}, bf16[2,2,2,2,96,128]{5,4,3,2,1,0:T(8,128)(2,1)S(1)}, u32[]{:S(2)}, u32[]{:S(2)}) collective-permute-start(bf16[2,2,2,2,96,128]{5,4,3,2,1,0:T(8,128)(2,1)S(1)} %collective-permute-done.11.refs_9_), channel_id=1, source_target_pairs={{0,14},{1,15},{2,0},{3,1},{4,2},{5,3},{6,4},{7,5},{8,6},{9,7},{10,... | collective-permute-start | bytes 1179656 | tf_op jit(solution)/shard_map/ppermute | solution.py:280
  49.4 16.9 %collective-permute-start.6 = (bf16[2,2,2,2,96,128]{5,4,3,2,1,0:T(8,128)(2,1)S(1)}, bf16[2,2,2,2,96,128]{5,4,3,2,1,0:T(8,128)(2,1)S(1)}, u32[]{:S(2)}, u32[]{:S(2)}) collective-permute-start(bf16[2,2,2,2,96,128]{5,4,3,2,1,0:T(8,128)(2,1)S(1)} %collective-permute-done.5.refs_6_), channel_id=1, source_target_pairs={{0,2},{1,3},{2,4},{3,5},{4,6},{5,7},{6,8},{7,9},{8,10},{9,11},{10,... | collective-permute-start | bytes 1179656 | tf_op jit(solution)/shard_map/ppermute | solution.py:280
  49.4 16.8 %collective-permute-start.2 = (bf16[2,2,256,128]{3,2,1,0:T(8,128)(2,1)S(1)}, bf16[2,2,256,128]{3,2,1,0:T(8,128)(2,1)S(1)}, u32[]{:S(2)}, u32[]{:S(2)}) collective-permute-start(bf16[2,2,256,128]{3,2,1,0:T(8,128)(2,1)S(1)} %get-tuple-element.36), channel_id=1, source_target_pairs={{0,17},{1,16},{2,19},{3,18},{4,21},{5,20},{6,23},{7,22},{8,25},{9,... | collective-permute-start | bytes 786440 | tf_op jit(solution)/shard_map/ppermute | solution.py:280
  57.6 21.4 %collective-permute-start.16 = (bf16[2,2,2,2,96,128]{5,4,3,2,1,0:T(8,128)(2,1)S(1)}, bf16[2,2,2,2,96,128]{5,4,3,2,1,0:T(8,128)(2,1)S(1)}, u32[]{:S(2)}, u32[]{:S(2)}) collective-permute-start(bf16[2,2,2,2,96,128]{5,4,3,2,1,0:T(8,128)(2,1)S(1)} %collective-permute-done.15.refs_7_), channel_id=1, source_target_pairs={{0,2},{1,3},{2,4},{3,5},{4,6},{5,7},{6,8},{7,9},{8,10},{9,11},{10,... | collective-permute-start | bytes 1179656 | tf_op jit(solution)/shard_map/ppermute | solution.py:280
  57.6 21.4 %collective-permute-start.19 = (bf16[2,2,2,2,96,128]{5,4,3,2,1,0:T(8,128)(2,1)S(1)}, bf16[2,2,2,2,96,128]{5,4,3,2,1,0:T(8,128)(2,1)S(1)}, u32[]{:S(2)}, u32[]{:S(2)}) collective-permute-start(bf16[2,2,2,2,96,128]{5,4,3,2,1,0:T(8,128)(2,1)S(1)} %collective-permute-done.18.refs_8_), channel_id=1, source_target_pairs={{0,14},{1,15},{2,0},{3,1},{4,2},{5,3},{6,4},{7,5},{8,6},{9,7},{10,... | collective-permute-start | bytes 1179656 | tf_op jit(solution)/shard_map/ppermute | solution.py:280
  62.8 19.6 %collective-permute-start.13 = (bf16[2,2,2,2,96,128]{5,4,3,2,1,0:T(8,128)(2,1)S(1)}, bf16[2,2,2,2,96,128]{5,4,3,2,1,0:T(8,128)(2,1)S(1)}, u32[]{:S(2)}, u32[]{:S(2)}) collective-permute-start(bf16[2,2,2,2,96,128]{5,4,3,2,1,0:T(8,128)(2,1)S(1)} %collective-permute-done.12.refs_9_), channel_id=1, source_target_pairs={{0,14},{1,15},{2,0},{3,1},{4,2},{5,3},{6,4},{7,5},{8,6},{9,7},{10,... | collective-permute-start | bytes 1179656 | tf_op jit(solution)/shard_map/ppermute | solution.py:280
  66.2 16.7 %collective-permute-start.7 = (bf16[2,2,2,2,96,128]{5,4,3,2,1,0:T(8,128)(2,1)S(1)}, bf16[2,2,2,2,96,128]{5,4,3,2,1,0:T(8,128)(2,1)S(1)}, u32[]{:S(2)}, u32[]{:S(2)}) collective-permute-start(bf16[2,2,2,2,96,128]{5,4,3,2,1,0:T(8,128)(2,1)S(1)} %collective-permute-done.6.refs_6_), channel_id=1, source_target_pairs={{0,2},{1,3},{2,4},{3,5},{4,6},{5,7},{6,8},{7,9},{8,10},{9,11},{10,... | collective-permute-start | bytes 1179656 | tf_op jit(solution)/shard_map/ppermute | solution.py:280
  85.6 15.0 %collective-permute-start.23 = (bf16[2,256,128]{2,1,0:T(8,128)(2,1)S(1)}, bf16[2,256,128]{2,1,0:T(8,128)(2,1)S(1)}, u32[]{:S(2)}, u32[]{:S(2)}) collective-permute-start(bf16[2,256,128]{2,1,0:T(8,128)(2,1)S(1)} %get-tuple-element.58), channel_id=1, source_target_pairs={{0,1},{1,0},{2,3},{3,2},{4,5},{5,4},{6,7},{7,6},{8,9},{9,8},{10,11... | collective-permute-start | bytes 393224 | tf_op jit(solution)/shard_map/ppermute | solution.py:280
  93.2 11.1 %collective-permute-start.24 = (bf16[2,256,128]{2,1,0:T(8,128)(2,1)S(1)}, bf16[2,256,128]{2,1,0:T(8,128)(2,1)S(1)}, u32[]{:S(2)}, u32[]{:S(2)}) collective-permute-start(bf16[2,256,128]{2,1,0:T(8,128)(2,1)S(1)} %get-tuple-element.59), channel_id=1, source_target_pairs={{0,16},{1,17},{2,18},{3,19},{4,20},{5,21},{6,22},{7,23},{8,24},{9,... | collective-permute-start | bytes 393224 | tf_op jit(solution)/shard_map/ppermute | solution.py:280
  94.4 9.9 %collective-permute-start.25 = (bf16[2,256,128]{2,1,0:T(8,128)(2,1)S(1)}, bf16[2,256,128]{2,1,0:T(8,128)(2,1)S(1)}, u32[]{:S(2)}, u32[]{:S(2)}) collective-permute-start(bf16[2,256,128]{2,1,0:T(8,128)(2,1)S(1)} %get-tuple-element.60), channel_id=1, source_target_pairs={{0,17},{1,16},{2,19},{3,18},{4,21},{5,20},{6,23},{7,22},{8,25},{9,... | collective-permute-start | bytes 393224 | tf_op jit(solution)/shard_map/ppermute | solution.py:280
  96.5 6.4 %copy-start.1 = (bf16[2,64,1024]{2,1,0:T(8,128)(2,1)S(1)}, bf16[2,64,1024]{2,1,0:T(8,128)(2,1)}, u32[]{:S(2)}) copy-start(bf16[2,64,1024]{2,1,0:T(8,128)(2,1)} %ck.3) | copy-start | bytes 786436
  96.5 6.4 %copy-start.2 = (bf16[2,32,1024]{2,1,0:T(8,128)(2,1)S(1)}, bf16[2,32,1024]{2,1,0:T(8,128)(2,1)}, u32[]{:S(2)}) copy-start(bf16[2,32,1024]{2,1,0:T(8,128)(2,1)} %sk.3) | copy-start | bytes 393220
  99.1 5.2 %collective-permute-start.20 = (bf16[2,256,128]{2,1,0:T(8,128)(2,1)S(1)}, bf16[2,256,128]{2,1,0:T(8,128)(2,1)S(1)}, u32[]{:S(2)}, u32[]{:S(2)}) collective-permute-start(bf16[2,256,128]{2,1,0:T(8,128)(2,1)S(1)} %get-tuple-element.48), channel_id=1, source_target_pairs={{0,1},{1,0},{2,3},{3,2},{4,5},{5,4},{6,7},{7,6},{8,9},{9,8},{10,11... | collective-permute-start | bytes 393224 | tf_op jit(solution)/shard_map/ppermute | solution.py:280
  99.4 6.2 %collective-permute-start.21 = (bf16[2,256,128]{2,1,0:T(8,128)(2,1)S(1)}, bf16[2,256,128]{2,1,0:T(8,128)(2,1)S(1)}, u32[]{:S(2)}, u32[]{:S(2)}) collective-permute-start(bf16[2,256,128]{2,1,0:T(8,128)(2,1)S(1)} %get-tuple-element.49), channel_id=1, source_target_pairs={{0,16},{1,17},{2,18},{3,19},{4,20},{5,21},{6,22},{7,23},{8,24},{9,... | collective-permute-start | bytes 393224 | tf_op jit(solution)/shard_map/ppermute | solution.py:280
  100.5 8.4 %collective-permute-start.22 = (bf16[2,256,128]{2,1,0:T(8,128)(2,1)S(1)}, bf16[2,256,128]{2,1,0:T(8,128)(2,1)S(1)}, u32[]{:S(2)}, u32[]{:S(2)}) collective-permute-start(bf16[2,256,128]{2,1,0:T(8,128)(2,1)S(1)} %get-tuple-element.50), channel_id=1, source_target_pairs={{0,17},{1,16},{2,19},{3,18},{4,21},{5,20},{6,23},{7,22},{8,25},{9,... | collective-permute-start | bytes 393224 | tf_op jit(solution)/shard_map/ppermute | solution.py:280

commit v2 on v1

--- a/solution.py
+++ b/solution.py
@@ -17,7 +17,6 @@
 QUAD = 4
 RING = 8
 KH = HK // QUAD
-PHASES = ((0, 7, 1), (6, 2), (5, 3), (4,))
 ATTEND_VMEM = 24 << 20
 SMALL_VMEM = 8 << 20
 SCALE = math.log2(math.e) / math.sqrt(DH)
@@ -139,22 +138,31 @@
     )(place, prefix_len, cache_keys, stretch_keys)
 
 
-def attend(s, place, prefix_len, queries, blocks, which, state, last, rows):
-    count = len(blocks)
+def attend(seqs, tiles, place, prefix_len, queries, parts, states, last, rows):
     tile = GROUP * rows
-    slots = QUAD // 2
-    pre = blocks[0][0].shape[4] - rows
-    half_rows = slots * rows
+    arrays = [x for _, _, held in parts for x in held]
+    pre = arrays[0].shape[4] - rows
+    sources = []
+    for d, slot, held in parts:
+        for x in held:
+            at = next(i for i, y in enumerate(arrays) if y is x)
+            for i in range(x.shape[0]):
+                sources.append((d, slot, at, i))
+                slot += 1
+    old_groups = [sources[i : i + DH // pre] for i in range(0, len(sources), DH // pre)]
+    new_groups = [sources[i : i + DH // rows] for i in range(0, len(sources), DH // rows)]
+    wide = len(old_groups) + len(new_groups)
+    jobs = [(i, r) for i in range(len(seqs)) for r in range(len(tiles))]
+    begun = states is not None
 
     def body(*refs):
-        place_ref, len_ref = refs[:2]
-        q_refs = refs[2 : 2 + QUAD]
-        half_refs = refs[2 + QUAD : 2 + QUAD + 2 * count]
-        rest = refs[2 + QUAD + 2 * count : -1]
-        score_ref = refs[-1]
-        if state is not None:
-            mixed_in, top_in = rest[:2]
-            rest = rest[2:]
+        refs = list(refs)
+        place_ref, len_ref, score_ref = refs.pop(0), refs.pop(0), refs.pop()
+        take = lambda n: [refs.pop(0) for _ in range(n)]
+        q_refs = {job: take(1)[0] for job in jobs}
+        kv_refs = [take(len(arrays)) for _ in seqs]
+        state_refs = [take(2) for _ in seqs] if begun else None
+        out_refs = [take(len(tiles) if last else 2) for _ in seqs]
         own = corner(place_ref)
         z = (place_ref[0] // 2) % RING
         lane = lax.broadcasted_iota(jnp.int32, (1, DH), 1)
@@ -163,117 +171,127 @@
             peer = own ^ slot
             return (peer // 2) * 16 + peer % 2 + ((z + d) % RING) * 2
 
-        def spread(first, width, d):
-            pos = shard(first, d) * width + lane
-            for k in range(1, DH // width):
-                pos = jnp.where(lane >= k * width, shard(first + k, d) * width + lane - k * width, pos)
+        def spread(group, width):
+            pos = shard(group[0][1], group[0][0]) * width + lane
+            for k, (d, slot, _, _) in enumerate(group[1:], 1):
+                pos = jnp.where(lane >= k * width, shard(slot, d) * width + lane - k * width, pos)
             return pos
 
-        def old_part(ref, kv):
-            return ref[:, kv, 0, 0, :pre, :].reshape(slots * pre, DH)
-
-        def new_part(ref, kv):
-            return ref[:, kv, 0, 0, pre:, :].reshape(half_rows, DH)
-
-        chunks = []
-        for b, d in enumerate(which):
-            for half in range(2):
-                ref = half_refs[2 * b + half]
-                fade = jnp.where(spread(half * slots, pre, d) < len_ref[s], 0.0, NEG)
-                chunks.append((lambda kv, ref=ref: old_part(ref, kv), fade, None))
-        for b, d in enumerate(which):
-            low, high = half_refs[2 * b : 2 * b + 2]
-            both = lambda kv, low=low, high=high: jnp.concatenate([new_part(low, kv), new_part(high, kv)], axis=0)
-            chunks.append((both, None, spread(0, rows, d)))
-        groups = [chunks[i : i + 2] for i in range(0, len(chunks), 2)]
-
-        def score(r):
-            q = q_refs[r][0, 0]
-            row_pos = shard(r, 0) * rows + lax.broadcasted_iota(jnp.int32, (tile, DH), 0) % rows
-            top = None
-            for g, group in enumerate(groups):
-                keys = jnp.concatenate([c[0](0) for c in group], axis=0)
-                part = lax.dot_general(
-                    q, keys, (((1,), (1,)), ((), ())), preferred_element_type=jnp.float32
-                )
-                for c, (_, fade, pos) in enumerate(group):
-                    piece = part[:, c * DH : (c + 1) * DH]
-                    if fade is not None:
-                        piece = piece + fade
-                    else:
-                        piece = jnp.where(pos <= row_pos, piece, NEG)
-                    score_ref[r % 2, 2 * g + c] = piece
-                    top = piece if top is None else jnp.maximum(top, piece)
+        old_pos = [spread(group, pre) for group in old_groups]
+        new_pos = [spread(group, rows) for group in new_groups]
+
+        def rows_of(i, kv, c):
+            if c < len(old_groups):
+                group, at = old_groups[c], slice(0, pre)
+            else:
+                group, at = new_groups[c - len(old_groups)], slice(pre, pre + rows)
+            return jnp.concatenate([kv_refs[i][x][k, kv, 0, 0, at, :] for _, _, x, k in group], axis=0)
+
+        fades = [[jnp.where(pos < len_ref[s], 0.0, NEG) for pos in old_pos] for s in seqs]
+        pairs = [range(c, min(c + 2, wide)) for c in range(0, wide, 2)]
+
+        def positions(job):
+            return shard(tiles[job[1]], 0) * rows + lax.broadcasted_iota(jnp.int32, (tile, DH), 0) % rows
+
+        def score(n, pair, row_pos, top):
+            i = jobs[n][0]
+            keys = jnp.concatenate([rows_of(i, 0, c) for c in pair], axis=0)
+            part = lax.dot_general(
+                q_refs[jobs[n]][0, 0], keys, (((1,), (1,)), ((), ())), preferred_element_type=jnp.float32
+            )
+            for k, c in enumerate(pair):
+                piece = part[:, k * DH : (k + 1) * DH]
+                if c < len(old_groups):
+                    piece = piece + fades[i][c]
+                else:
+                    piece = jnp.where(new_pos[c - len(old_groups)] <= row_pos, piece, NEG)
+                score_ref[n % 2, c] = piece
+                top = piece if top is None else jnp.maximum(top, piece)
             return top
 
-        def mix(r, top):
+        def settle(job, top):
+            top = jnp.broadcast_to(jnp.max(top, axis=-1, keepdims=True), (tile, DH))
+            if begun:
+                top = jnp.maximum(top, state_refs[job[0]][1][0, job[1] * tile : (job[1] + 1) * tile, :])
+            return top
+
+        def mix(n, pair, top, mixed):
+            weights = [jnp.exp2((score_ref[n % 2, c] - top) * SCALE).astype(jnp.bfloat16) for c in pair]
+            values = jnp.concatenate([rows_of(jobs[n][0], 1, c) for c in pair], axis=0)
+            part = jnp.dot(
+                jnp.concatenate(weights, axis=1),
+                jnp.concatenate([values, jnp.ones_like(values)], axis=1),
+                preferred_element_type=jnp.float32,
+            )
+            return part if mixed is None else mixed + part
+
+        def finish(job, top, mixed):
+            i, r = job
             at = slice(r * tile, (r + 1) * tile)
-            top = jnp.broadcast_to(jnp.max(top, axis=-1, keepdims=True), (tile, DH))
-            if state is not None:
-                old_top = top_in[0, at, :]
-                top = jnp.maximum(top, old_top)
-            mixed = None
-            for g, group in enumerate(groups):
-                weights = [
-                    jnp.exp2((score_ref[r % 2, 2 * g + c] - top) * SCALE).astype(jnp.bfloat16)
-                    for c in range(len(group))
-                ]
-                values = jnp.concatenate([c[0](1) for c in group], axis=0)
-                part = jnp.dot(
-                    jnp.concatenate(weights, axis=1),
-                    jnp.concatenate([values, jnp.ones_like(values)], axis=1),
-                    preferred_element_type=jnp.float32,
-                )
-                mixed = part if mixed is None else mixed + part
             total, mixed = mixed[:, DH:], mixed[:, :DH]
-            if state is not None:
-                shrink = jnp.exp2((old_top - top) * SCALE)
+            if begun:
+                mixed_in, top_in = state_refs[i]
+                shrink = jnp.exp2((top_in[0, at, :] - top) * SCALE)
                 mixed = mixed + mixed_in[0, at, :DH] * shrink
                 total = total + mixed_in[0, at, DH:] * shrink
             if last:
-                rest[r][0] = (mixed / total).astype(jnp.bfloat16)
+                out_refs[i][r][0] = (mixed / total).astype(jnp.bfloat16)
             else:
-                rest[0][0, at, :DH] = mixed
-                rest[0][0, at, DH:] = total
-                rest[1][0, at, :] = top
-
-        tops = score(0)
-        for r in range(QUAD):
-            following = score(r + 1) if r + 1 < QUAD else None
-            mix(r, tops)
-            tops = following
-
-    half_shape = (slots, 2, 1, 1) + blocks[0][0].shape[4:]
+                out_refs[i][0][0, at, :DH] = mixed
+                out_refs[i][0][0, at, DH:] = total
+                out_refs[i][1][0, at, :] = top
+
+        top = None
+        for pair in pairs:
+            top = score(0, pair, positions(jobs[0]), top)
+        for n, job in enumerate(jobs):
+            top = settle(job, top)
+            following, mixed = None, None
+            for pair in pairs:
+                if n + 1 < len(jobs):
+                    following = score(n + 1, pair, positions(jobs[n + 1]), following)
+                mixed = mix(n, pair, top, mixed)
+            finish(job, top, mixed)
+            top = following
+
+    part = tiles[0] // len(tiles)
     state_specs = [
-        pl.BlockSpec((1, QUAD * tile, 2 * DH), lambda h: (h, 0, 0)),
-        pl.BlockSpec((1, QUAD * tile, DH), lambda h: (h, 0, 0)),
+        pl.BlockSpec((1, len(tiles) * tile, 2 * DH), lambda h: (h, part, 0)),
+        pl.BlockSpec((1, len(tiles) * tile, DH), lambda h: (h, part, 0)),
     ]
     in_specs = [pl.BlockSpec(memory_space=pltpu.SMEM)] * 2
-    in_specs += [pl.BlockSpec((1, 1, tile, DH), lambda h: (s, h, 0, 0))] * QUAD
-    in_specs += [pl.BlockSpec(half_shape, lambda h: (0, 0, s, h, 0, 0))] * (2 * count)
-    operands = [place, prefix_len, *queries, *[half for block in blocks for half in block]]
-    if state is not None:
-        in_specs += state_specs
-        operands += list(state)
+    operands = [place, prefix_len]
+    for i, r in jobs:
+        in_specs.append(pl.BlockSpec((1, 1, tile, DH), lambda h, s=seqs[i]: (s, h, 0, 0)))
+        operands.append(queries[tiles[r]])
+    for s in seqs:
+        in_specs += [
+            pl.BlockSpec(x.shape[:2] + (1, 1) + x.shape[4:], lambda h, s=s: (0, 0, s, h, 0, 0)) for x in arrays
+        ]
+        operands += arrays
+    if begun:
+        in_specs += state_specs * len(seqs)
+        operands += [x for s in seqs for x in states[s]]
     if last:
-        out_specs = [pl.BlockSpec((1, tile, DH), lambda h: (h, 0, 0))] * QUAD
-        out_shape = [jax.ShapeDtypeStruct((KH, tile, DH), jnp.bfloat16)] * QUAD
+        out_specs = [pl.BlockSpec((1, tile, DH), lambda h: (h, 0, 0))] * len(jobs)
+        out_shape = [jax.ShapeDtypeStruct((KH, tile, DH), jnp.bfloat16)] * len(jobs)
     else:
-        out_specs = state_specs
-        out_shape = [jax.ShapeDtypeStruct((KH, QUAD * tile, w), jnp.float32) for w in (2 * DH, DH)]
-    wide = count * (QUAD * (pre + rows)) // DH
-    pairs = KH * QUAD * tile * wide * DH
-    return pl.pallas_call(
+        out_specs = state_specs * len(seqs)
+        out_shape = [jax.ShapeDtypeStruct((KH, QUAD * tile, w), jnp.float32) for w in (2 * DH, DH)] * len(seqs)
+    count = KH * len(jobs) * tile * wide * DH
+    outs = pl.pallas_call(
         body,
         grid=(KH,),
         in_specs=in_specs,
         out_specs=out_specs,
         out_shape=out_shape,
         scratch_shapes=[pltpu.VMEM((2, wide, tile, DH), jnp.float32)],
-        cost_estimate=pl.CostEstimate(flops=4 * DH * pairs, transcendentals=pairs, bytes_accessed=4 << 20),
+        cost_estimate=pl.CostEstimate(flops=4 * DH * count, transcendentals=count, bytes_accessed=4 << 20),
         compiler_params=pltpu.CompilerParams(vmem_limit_bytes=ATTEND_VMEM),
         name="attend",
     )(*operands)
+    each = len(outs) // len(seqs)
+    return {s: outs[i * each : (i + 1) * each] for i, s in enumerate(seqs)}
 
 
 def send(array, perm):
@@ -290,24 +308,34 @@
     q_tiles = [packed[0]] + [send(packed[r], quad_perm(r)) for r in range(1, QUAD)]
     prefix_bounds, stretch_bounds = bounds(place, prefix_len, cache_keys, stretch_keys)
 
+    half = RING // 2
     rings = []
     for n in range(2):
-        ring = {0: jnp.stack(got[2 * n : 2 * n + 2])}
-        for step in range(1, RING // 2 + 1):
-            if step < RING // 2 or n == 0:
-                ring[-step % RING] = send(ring[(1 - step) % RING], ring_perm(1))
-            if step < RING // 2 or n == 1:
-                ring[step] = send(ring[step - 1], ring_perm(-1))
+        ring = {0: [jnp.stack(got[2 * n : 2 * n + 2])]}
+        for step in range(1, half):
+            ring[-step % RING] = [send(ring[(1 - step) % RING][0], ring_perm(1))]
+            ring[step] = [send(ring[step - 1][0], ring_perm(-1))]
         rings.append(ring)
-
-    sent = []
+    for n in range(2):
+        rings[n][half] = [send(rings[n][half + 1][0][:1], ring_perm(1)), send(rings[n][half - 1][0][1:], ring_perm(-1))]
+
+    whole = lambda *ds: [(d, 0, rings[0][d] + rings[1][d]) for d in ds]
+    common = (place, prefix_len, q_tiles)
+    every = tuple(range(QUAD))
+    states = {}
     for s in range(seqs):
-        state = None
-        for n, which in enumerate(PHASES):
-            last = n + 1 == len(PHASES)
-            blocks = [(rings[0][d], rings[1][d]) for d in which]
-            state = attend(s, place, prefix_len, q_tiles, blocks, which, state, last, rows)
-        sent.append([state[0]] + [send(state[r], quad_perm(r)) for r in range(1, QUAD)])
+        states.update(attend((s,), every, *common, whole(0, 7, 1), None, False, rows))
+    states = attend((0, 1), every, *common, whole(6, 2), states, False, rows)
+    for n in range(2):
+        held = [(d, 2 * n, rings[n][d]) for d in (5, 3)]
+        states = attend((0, 1), every, *common, held, states, False, rows)
+
+    sent = [[None] * QUAD for _ in range(seqs)]
+    for group, tiles in (((1,), (2, 3)), ((0,), (2, 3)), ((0, 1), (0, 1))):
+        done = attend(group, tiles, *common, whole(half), states, True, rows)
+        for s in group:
+            for r, out in zip(tiles, done[s]):
+                sent[s][r] = send(out, quad_perm(r)) if r else out
     attention = unpack_out(place, sent, rows)
     return attention, prefix_bounds, stretch_bounds
 

time: 112 us -> 110 us (0.982)
  waiting for transfers between devices: 37 us -> 31.3 us
  starting transfers between devices: 39.8 us -> 41.9 us
  Pallas kernels: 32.4 us -> 33.8 us
    ppermute x26 -> x28, waiting for transfers between devices: 37 us -> 31.3 us  [send(): return lax.ppermute(array, 'seq', perm)]
    ppermute x26 -> x28, starting transfers between devices: 39.8 us -> 41.9 us  [send(): return lax.ppermute(array, 'seq', perm)]
    pallas_call x8, Pallas kernels: 28.1 us -> 29.5 us  [attend(): pl.pallas_call(body, grid=(KH,), in_specs=in_specs, out_specs=out_specs,...]
  transfers between devices with their start and end apart: 26 -> 28, of which waited for: 11 -> 8; matrix products, arithmetic and copies ran while one was open for 0% -> 0% of each run, Pallas kernels for 25% -> 27%
where the time goes in v2:
time: 110 us; the launch traced here: 108 us
  starting transfers between devices  41.9 us (38%)
  Pallas kernels  33.8 us (31%)
  waiting for transfers between devices  31.3 us (28%)
    ppermute x28, starting transfers between devices, send(): return lax.ppermute(array, 'seq', perm)  41.9 us
    ppermute x28, waiting for transfers between devices, send(): return lax.ppermute(array, 'seq', perm)  31.3 us
    pallas_call x8, Pallas kernels, attend(): pl.pallas_call(body, grid=(KH,), in_specs=in_specs, out_specs=out_specs,...  29.5 us
  transfers between devices with their start and end apart: 28, of which 8 were waited for; matrix products, arithmetic and copies ran while one was open for 0% of the time, Pallas kernels for 27%

profile of v2, /device:TPU:7, one launch (start us, length us, event | category | flops | bytes accessed | tf_op | source)
XLA Modules:
  0.0 108.1 jit_solution(6962284011213446448)
XLA Ops:
  0.7 1.4 %pack_kv.1 = (bf16[2,2,2,96,128]{4,3,2,1,0:T(8,128)(2,1)S(1)}, bf16[2,2,2,96,128]{4,3,2,1,0:T(8,128)(2,1)S(1)}, bf16[2,2,2,96,128]{4,3,2,1,0:T(8,128)(2,1)S(1)}, bf16[2,2,2,96,128]{4,3,2,1,0:T(8,128)(2,1)S(1)}) custom-call(s32[1]{0:T(128)} %bitcast.place_ref.refs_0_, bf16[2,64,1024]{2,1,0:T(8,128)(2,1)} %ck.3, bf16[2,64,1024]{2,1,0:T(8,128)(2,1)} %cv.1, ...), custom_call_target="tpu_custom_call" | custom-call | tf_op jit(solution)/shard_map/pack_kv/pallas_call | solution.py:52
  2.1 1.2 %collective-permute-start.10 = (bf16[2,2,2,96,128]{4,3,2,1,0:T(8,128)(2,1)S(1)}, bf16[2,2,2,96,128]{4,3,2,1,0:T(8,128)(2,1)S(1)}, u32[]{:S(2)}, u32[]{:S(2)}) collective-permute-start(bf16[2,2,2,96,128]{4,3,2,1,0:T(8,128)(2,1)S(1)} %get-tuple-element.41), channel_id=1, source_target_pairs={{0,16},{1,17},{2,18},{3,19},{4,20},{5,21},{6,22},{7,23},{8,24},{9,... | collective-permute-start | bytes 589832 | tf_op jit(solution)/shard_map/ppermute | solution.py:298
  3.3 2.7 %collective-permute-start.11 = (bf16[2,2,2,96,128]{4,3,2,1,0:T(8,128)(2,1)S(1)}, bf16[2,2,2,96,128]{4,3,2,1,0:T(8,128)(2,1)S(1)}, u32[]{:S(2)}, u32[]{:S(2)}) collective-permute-start(bf16[2,2,2,96,128]{4,3,2,1,0:T(8,128)(2,1)S(1)} %get-tuple-element.42), channel_id=1, source_target_pairs={{0,17},{1,16},{2,19},{3,18},{4,21},{5,20},{6,23},{7,22},{8,25},{9,... | collective-permute-start | bytes 589832 | tf_op jit(solution)/shard_map/ppermute | solution.py:298
  5.9 0.0 collective-permute-start.1
  6.0 3.5 %collective-permute-done.10 = bf16[2,2,2,96,128]{4,3,2,1,0:T(8,128)(2,1)S(1)} collective-permute-done((bf16[2,2,2,96,128]{4,3,2,1,0:T(8,128)(2,1)S(1)}, bf16[2,2,2,96,128]{4,3,2,1,0:T(8,128)(2,1)S(1)}, u32[]{:S(2)}, u32[]{:S(2)}) %collective-permute-start.10) | collective-permute-done | bytes 196640 | tf_op jit(solution)/shard_map/ppermute | solution.py:298
  9.4 5.1 %collective-permute-done.11 = bf16[2,2,2,96,128]{4,3,2,1,0:T(8,128)(2,1)S(1)} collective-permute-done((bf16[2,2,2,96,128]{4,3,2,1,0:T(8,128)(2,1)S(1)}, bf16[2,2,2,96,128]{4,3,2,1,0:T(8,128)(2,1)S(1)}, u32[]{:S(2)}, u32[]{:S(2)}) %collective-permute-start.11) | collective-permute-done | bytes 196640 | tf_op jit(solution)/shard_map/ppermute | solution.py:298
  14.5 1.7 %collective-permute-start.12 = (bf16[2,2,2,2,96,128]{5,4,3,2,1,0:T(8,128)(2,1)S(1)}, bf16[2,2,2,2,96,128]{5,4,3,2,1,0:T(8,128)(2,1)S(1)}, u32[]{:S(2)}, u32[]{:S(2)}) collective-permute-start(bf16[2,2,2,2,96,128]{5,4,3,2,1,0:T(8,128)(2,1)S(1)} %pad_maximum_fusion.1.refs_7_), channel_id=1, source_target_pairs={{0,2},{1,3},{2,4},{3,5},{4,6},{5,7},{6,8},{7,9},{8,10},{9,11},{10,... | collective-permute-start | bytes 1179656 | tf_op jit(solution)/shard_map/ppermute | solution.py:298
  16.2 4.0 %collective-permute-start.16 = (bf16[2,2,2,2,96,128]{5,4,3,2,1,0:T(8,128)(2,1)S(1)}, bf16[2,2,2,2,96,128]{5,4,3,2,1,0:T(8,128)(2,1)S(1)}, u32[]{:S(2)}, u32[]{:S(2)}) collective-permute-start(bf16[2,2,2,2,96,128]{5,4,3,2,1,0:T(8,128)(2,1)S(1)} %pad_maximum_fusion.1.refs_7_), channel_id=1, source_target_pairs={{0,14},{1,15},{2,0},{3,1},{4,2},{5,3},{6,4},{7,5},{8,6},{9,7},{10,... | collective-permute-start | bytes 1179656 | tf_op jit(solution)/shard_map/ppermute | solution.py:298
  20.3 0.0 collective-permute-done.1
  20.3 0.1 collective-permute-start.2
  20.4 2.7 %collective-permute-start.6 = (bf16[2,2,2,2,96,128]{5,4,3,2,1,0:T(8,128)(2,1)S(1)}, bf16[2,2,2,2,96,128]{5,4,3,2,1,0:T(8,128)(2,1)S(1)}, u32[]{:S(2)}, u32[]{:S(2)}) collective-permute-start(bf16[2,2,2,2,96,128]{5,4,3,2,1,0:T(8,128)(2,1)S(1)} %pad_maximum_fusion.refs_6_), channel_id=1, source_target_pairs={{0,14},{1,15},{2,0},{3,1},{4,2},{5,3},{6,4},{7,5},{8,6},{9,7},{10,... | collective-permute-start | bytes 1179656 | tf_op jit(solution)/shard_map/ppermute | solution.py:298
  23.1 0.3 pack_q.1
  23.4 1.2 %collective-permute-start.20 = (bf16[2,2,256,128]{3,2,1,0:T(8,128)(2,1)S(1)}, bf16[2,2,256,128]{3,2,1,0:T(8,128)(2,1)S(1)}, u32[]{:S(2)}, u32[]{:S(2)}) collective-permute-start(bf16[2,2,256,128]{3,2,1,0:T(8,128)(2,1)S(1)} %get-tuple-element.43), channel_id=1, source_target_pairs={{0,16},{1,17},{2,18},{3,19},{4,20},{5,21},{6,22},{7,23},{8,24},{9,... | collective-permute-start | bytes 786440 | tf_op jit(solution)/shard_map/ppermute | solution.py:298
  24.6 5.3 %collective-permute-done.12.refs_9_ = bf16[2,2,2,2,96,128]{5,4,3,2,1,0:T(8,128)(2,1)S(1)} collective-permute-done((bf16[2,2,2,2,96,128]{5,4,3,2,1,0:T(8,128)(2,1)S(1)}, bf16[2,2,2,2,96,128]{5,4,3,2,1,0:T(8,128)(2,1)S(1)}, u32[]{:S(2)}, u32[]{:S(2)}) %collective-permute-start.12) | collective-permute-done | bytes 393248 | tf_op jit(solution)/shard_map/ppermute | solution.py:298
  29.8 0.0 collective-permute-start.13
  29.9 0.0 collective-permute-done.16.refs_11_
  29.9 2.7 %collective-permute-start.17 = (bf16[2,2,2,2,96,128]{5,4,3,2,1,0:T(8,128)(2,1)S(1)}, bf16[2,2,2,2,96,128]{5,4,3,2,1,0:T(8,128)(2,1)S(1)}, u32[]{:S(2)}, u32[]{:S(2)}) collective-permute-start(bf16[2,2,2,2,96,128]{5,4,3,2,1,0:T(8,128)(2,1)S(1)} %collective-permute-done.16.refs_11_), channel_id=1, source_target_pairs={{0,14},{1,15},{2,0},{3,1},{4,2},{5,3},{6,4},{7,5},{8,6},{9,7},{10,... | collective-permute-start | bytes 1179656 | tf_op jit(solution)/shard_map/ppermute | solution.py:298
  32.6 5.7 %collective-permute-done.2.refs_8_ = bf16[2,2,2,2,96,128]{5,4,3,2,1,0:T(8,128)(2,1)S(1)} collective-permute-done((bf16[2,2,2,2,96,128]{5,4,3,2,1,0:T(8,128)(2,1)S(1)}, bf16[2,2,2,2,96,128]{5,4,3,2,1,0:T(8,128)(2,1)S(1)}, u32[]{:S(2)}, u32[]{:S(2)}) %collective-permute-start.2) | collective-permute-done | bytes 393248 | tf_op jit(solution)/shard_map/ppermute | solution.py:298
  38.3 2.7 %collective-permute-start.7 = (bf16[2,2,2,2,96,128]{5,4,3,2,1,0:T(8,128)(2,1)S(1)}, bf16[2,2,2,2,96,128]{5,4,3,2,1,0:T(8,128)(2,1)S(1)}, u32[]{:S(2)}, u32[]{:S(2)}) collective-permute-start(bf16[2,2,2,2,96,128]{5,4,3,2,1,0:T(8,128)(2,1)S(1)} %collective-permute-done.6.refs_10_), channel_id=1, source_target_pairs={{0,14},{1,15},{2,0},{3,1},{4,2},{5,3},{6,4},{7,5},{8,6},{9,7},{10,... | collective-permute-start | bytes 1179656 | tf_op jit(solution)/shard_map/ppermute | solution.py:298
  41.0 1.7 %collective-permute-start.21 = (bf16[2,2,256,128]{3,2,1,0:T(8,128)(2,1)S(1)}, bf16[2,2,256,128]{3,2,1,0:T(8,128)(2,1)S(1)}, u32[]{:S(2)}, u32[]{:S(2)}) collective-permute-start(bf16[2,2,256,128]{3,2,1,0:T(8,128)(2,1)S(1)} %get-tuple-element.44), channel_id=1, source_target_pairs={{0,17},{1,16},{2,19},{3,18},{4,21},{5,20},{6,23},{7,22},{8,25},{9,... | collective-permute-start | bytes 786440 | tf_op jit(solution)/shard_map/ppermute | solution.py:298
  42.7 8.7 %collective-permute-done.21.refs_5_.refs_9_.refs_3_ = bf16[2,2,256,128]{3,2,1,0:T(8,128)(2,1)S(1)} collective-permute-done((bf16[2,2,256,128]{3,2,1,0:T(8,128)(2,1)S(1)}, bf16[2,2,256,128]{3,2,1,0:T(8,128)(2,1)S(1)}, u32[]{:S(2)}, u32[]{:S(2)}) %collective-permute-start.21) | collective-permute-done | bytes 262176 | tf_op jit(solution)/shard_map/ppermute | solution.py:298
  51.4 0.4 collective-permute-start
  51.8 2.7 %collective-permute-start.18 = (bf16[2,2,2,2,96,128]{5,4,3,2,1,0:T(8,128)(2,1)S(1)}, bf16[2,2,2,2,96,128]{5,4,3,2,1,0:T(8,128)(2,1)S(1)}, u32[]{:S(2)}, u32[]{:S(2)}) collective-permute-start(bf16[2,2,2,2,96,128]{5,4,3,2,1,0:T(8,128)(2,1)S(1)} %collective-permute-done.17.refs_13_.refs_17_), channel_id=1, source_target_pairs={{0,14},{1,15},{2,0},{3,1},{4,2},{5,3},{6,4},{7,5},{8,6},{9,7},{10,... | collective-permute-start | bytes 1179656 | tf_op jit(solution)/shard_map/ppermute | solution.py:298
  54.5 0.1 collective-permute-done.3.refs_10_.refs_14_
  54.6 0.0 collective-permute-start.4
  54.6 3.3 %collective-permute-start.8 = (bf16[2,2,2,2,96,128]{5,4,3,2,1,0:T(8,128)(2,1)S(1)}, bf16[2,2,2,2,96,128]{5,4,3,2,1,0:T(8,128)(2,1)S(1)}, u32[]{:S(2)}, u32[]{:S(2)}) collective-permute-start(bf16[2,2,2,2,96,128]{5,4,3,2,1,0:T(8,128)(2,1)S(1)} %collective-permute-done.7.refs_12_.refs_16_), channel_id=1, source_target_pairs={{0,14},{1,15},{2,0},{3,1},{4,2},{5,3},{6,4},{7,5},{8,6},{9,7},{10,... | collective-permute-start | bytes 1179656 | tf_op jit(solution)/shard_map/ppermute | solution.py:298
  57.9 4.7 %attend.9 = (f32[2,1024,256]{2,1,0:T(8,128)S(1)}, f32[2,1024,128]{2,1,0:T(8,128)S(1)}) custom-call(s32[1]{0:T(128)} %bitcast.place_ref.refs_0_, s32[2]{0:T(128)S(1)} %copy-done.3, bf16[2,2,256,128]{3,2,1,0:T(8,128)(2,1)S(1)} %get-tuple-element.37.refs_2_.refs_6_.refs_4_, bf16[2,2,256,128]{3,2,1,0:T(8,128)(2,1)S(1)} %collective-permute-done.refs_3_.refs_7_.refs_5_, ...), custom_call_target="tpu_custom_call" | custom-call | flops 1207959552 | bytes 4194304 | tf_op jit(solution)/shard_map/attend/pallas_call | solution.py:282
  62.6 4.7 %attend.8 = (f32[2,1024,256]{2,1,0:T(8,128)S(1)}, f32[2,1024,128]{2,1,0:T(8,128)S(1)}) custom-call(s32[1]{0:T(128)} %bitcast.place_ref.refs_0_, s32[2]{0:T(128)S(1)} %copy-done.3, bf16[2,2,256,128]{3,2,1,0:T(8,128)(2,1)S(1)} %get-tuple-element.37.refs_2_.refs_6_.refs_4_, bf16[2,2,256,128]{3,2,1,0:T(8,128)(2,1)S(1)} %collective-permute-done.refs_3_.refs_7_.refs_5_, ...), custom_call_target="tpu_custom_call" | custom-call | flops 1207959552 | bytes 4194304 | tf_op jit(solution)/shard_map/attend/pallas_call | solution.py:282
  67.3 0.1 collective-permute-start.15
  67.4 2.7 %collective-permute-start.19 = (bf16[1,2,2,2,96,128]{5,4,3,2,1,0:T(8,128)(2,1)S(1)}, bf16[1,2,2,2,96,128]{5,4,3,2,1,0:T(8,128)(2,1)S(1)}, u32[]{:S(2)}, u32[]{:S(2)}) collective-permute-start(bf16[1,2,2,2,96,128]{5,4,3,2,1,0:T(8,128)(2,1)S(1)} %slice.19), channel_id=1, source_target_pairs={{0,14},{1,15},{2,0},{3,1},{4,2},{5,3},{6,4},{7,5},{8,6},{9,7},{10,... | collective-permute-start | bytes 589832 | tf_op jit(solution)/shard_map/ppermute | solution.py:298
  70.2 1.9 %collective-permute-done.4.refs_10_.refs_12_ = bf16[2,2,2,2,96,128]{5,4,3,2,1,0:T(8,128)(2,1)S(1)} collective-permute-done((bf16[2,2,2,2,96,128]{5,4,3,2,1,0:T(8,128)(2,1)S(1)}, bf16[2,2,2,2,96,128]{5,4,3,2,1,0:T(8,128)(2,1)S(1)}, u32[]{:S(2)}, u32[]{:S(2)}) %collective-permute-start.4) | collective-permute-done | bytes 393248 | tf_op jit(solution)/shard_map/ppermute | solution.py:298
  72.1 0.1 collective-permute-start.5
  72.2 2.9 %collective-permute-start.9 = (bf16[1,2,2,2,96,128]{5,4,3,2,1,0:T(8,128)(2,1)S(1)}, bf16[1,2,2,2,96,128]{5,4,3,2,1,0:T(8,128)(2,1)S(1)}, u32[]{:S(2)}, u32[]{:S(2)}) collective-permute-start(bf16[1,2,2,2,96,128]{5,4,3,2,1,0:T(8,128)(2,1)S(1)} %slice.17), channel_id=1, source_target_pairs={{0,14},{1,15},{2,0},{3,1},{4,2},{5,3},{6,4},{7,5},{8,6},{9,7},{10,... | collective-permute-start | bytes 589832 | tf_op jit(solution)/shard_map/ppermute | solution.py:298
  75.1 5.3 %attend.10 = (f32[2,1024,256]{2,1,0:T(8,128)S(1)}, f32[2,1024,128]{2,1,0:T(8,128)S(1)}, f32[2,1024,256]{2,1,0:T(8,128)S(1)}, f32[2,1024,128]{2,1,0:T(8,128)S(1)}) custom-call(s32[1]{0:T(128)} %bitcast.place_ref.refs_0_, s32[2]{0:T(128)S(1)} %copy-done.3, bf16[2,2,256,128]{3,2,1,0:T(8,128)(2,1)S(1)} %get-tuple-element.37.refs_2_.refs_6_.refs_4_, ...), custom_call_target="tpu_custom_call" | custom-call | flops 1610612736 | bytes 4194304 | tf_op jit(solution)/shard_map/attend/pallas_call | solution.py:282
  80.4 4.1 %attend.11 = (f32[2,1024,256]{2,1,0:T(8,128)S(1)}, f32[2,1024,128]{2,1,0:T(8,128)S(1)}, f32[2,1024,256]{2,1,0:T(8,128)S(1)}, f32[2,1024,128]{2,1,0:T(8,128)S(1)}) custom-call(s32[1]{0:T(128)} %bitcast.place_ref.refs_0_, s32[2]{0:T(128)S(1)} %copy-done.3, bf16[2,2,256,128]{3,2,1,0:T(8,128)(2,1)S(1)} %get-tuple-element.37.refs_2_.refs_6_.refs_4_, ...), custom_call_target="tpu_custom_call" | custom-call | flops 805306368 | bytes 4194304 | tf_op jit(solution)/shard_map/attend/pallas_call | solution.py:282
  84.6 4.1 %attend.12 = (f32[2,1024,256]{2,1,0:T(8,128)S(1)}, f32[2,1024,128]{2,1,0:T(8,128)S(1)}, f32[2,1024,256]{2,1,0:T(8,128)S(1)}, f32[2,1024,128]{2,1,0:T(8,128)S(1)}) custom-call(s32[1]{0:T(128)} %bitcast.place_ref.refs_0_, s32[2]{0:T(128)S(1)} %copy-done.3, bf16[2,2,256,128]{3,2,1,0:T(8,128)(2,1)S(1)} %get-tuple-element.37.refs_2_.refs_6_.refs_4_, ...), custom_call_target="tpu_custom_call" | custom-call | flops 805306368 | bytes 4194304 | tf_op jit(solution)/shard_map/attend/pallas_call | solution.py:282
  88.8 2.0 %attend.15 = (bf16[2,256,128]{2,1,0:T(8,128)(2,1)S(1)}, bf16[2,256,128]{2,1,0:T(8,128)(2,1)S(1)}) custom-call(s32[1]{0:T(128)} %bitcast.place_ref.refs_0_, s32[2]{0:T(128)S(1)} %copy-done.3, bf16[2,2,256,128]{3,2,1,0:T(8,128)(2,1)S(1)} %collective-permute-done.20.refs_4_.refs_8_.refs_2_, ...), custom_call_target="tpu_custom_call" | custom-call | flops 201326592 | bytes 4194304 | tf_op jit(solution)/shard_map/attend/pallas_call | solution.py:282
  90.7 1.2 %collective-permute-start.26 = (bf16[2,256,128]{2,1,0:T(8,128)(2,1)S(1)}, bf16[2,256,128]{2,1,0:T(8,128)(2,1)S(1)}, u32[]{:S(2)}, u32[]{:S(2)}) collective-permute-start(bf16[2,256,128]{2,1,0:T(8,128)(2,1)S(1)} %get-tuple-element.67), channel_id=1, source_target_pairs={{0,16},{1,17},{2,18},{3,19},{4,20},{5,21},{6,22},{7,23},{8,24},{9,... | collective-permute-start | bytes 393224 | tf_op jit(solution)/shard_map/ppermute | solution.py:298
  91.9 4.1 %collective-permute-start.27 = (bf16[2,256,128]{2,1,0:T(8,128)(2,1)S(1)}, bf16[2,256,128]{2,1,0:T(8,128)(2,1)S(1)}, u32[]{:S(2)}, u32[]{:S(2)}) collective-permute-start(bf16[2,256,128]{2,1,0:T(8,128)(2,1)S(1)} %get-tuple-element.68), channel_id=1, source_target_pairs={{0,17},{1,16},{2,19},{3,18},{4,21},{5,20},{6,23},{7,22},{8,25},{9,... | collective-permute-start | bytes 393224 | tf_op jit(solution)/shard_map/ppermute | solution.py:298
  96.0 1.9 %attend.14 = (bf16[2,256,128]{2,1,0:T(8,128)(2,1)S(1)}, bf16[2,256,128]{2,1,0:T(8,128)(2,1)S(1)}) custom-call(s32[1]{0:T(128)} %bitcast.place_ref.refs_0_, s32[2]{0:T(128)S(1)} %copy-done.3, bf16[2,2,256,128]{3,2,1,0:T(8,128)(2,1)S(1)} %collective-permute-done.20.refs_4_.refs_8_.refs_2_, ...), custom_call_target="tpu_custom_call" | custom-call | flops 201326592 | bytes 4194304 | tf_op jit(solution)/shard_map/attend/pallas_call | solution.py:282
  98.0 1.2 %collective-permute-start.23 = (bf16[2,256,128]{2,1,0:T(8,128)(2,1)S(1)}, bf16[2,256,128]{2,1,0:T(8,128)(2,1)S(1)}, u32[]{:S(2)}, u32[]{:S(2)}) collective-permute-start(bf16[2,256,128]{2,1,0:T(8,128)(2,1)S(1)} %get-tuple-element.63), channel_id=1, source_target_pairs={{0,16},{1,17},{2,18},{3,19},{4,20},{5,21},{6,22},{7,23},{8,24},{9,... | collective-permute-start | bytes 393224 | tf_op jit(solution)/shard_map/ppermute | solution.py:298
  99.2 0.3 collective-permute-start.24
  99.5 2.7 %attend.13 = (bf16[2,256,128]{2,1,0:T(8,128)(2,1)S(1)}, bf16[2,256,128]{2,1,0:T(8,128)(2,1)S(1)}, bf16[2,256,128]{2,1,0:T(8,128)(2,1)S(1)}, bf16[2,256,128]{2,1,0:T(8,128)(2,1)S(1)}) custom-call(s32[1]{0:T(128)} %bitcast.place_ref.refs_0_, s32[2]{0:T(128)S(1)} %copy-done.3, bf16[2,2,256,128]{3,2,1,0:T(8,128)(2,1)S(1)} %get-tuple-element.37.refs_2_.refs_6_.refs_4_, ...), custom_call_target="tpu_custom_call" | custom-call | flops 402653184 | bytes 4194304 | tf_op jit(solution)/shard_map/attend/pallas_call | solution.py:282
  102.1 2.0 %collective-permute-start.22 = (bf16[2,256,128]{2,1,0:T(8,128)(2,1)S(1)}, bf16[2,256,128]{2,1,0:T(8,128)(2,1)S(1)}, u32[]{:S(2)}, u32[]{:S(2)}) collective-permute-start(bf16[2,256,128]{2,1,0:T(8,128)(2,1)S(1)} %get-tuple-element.62), channel_id=1, source_target_pairs={{0,1},{1,0},{2,3},{3,2},{4,5},{5,4},{6,7},{7,6},{8,9},{9,8},{10,11... | collective-permute-start | bytes 393224 | tf_op jit(solution)/shard_map/ppermute | solution.py:298
  104.2 0.1 collective-permute-start.25
  104.3 1.4 %page_bounds.1 = (bf16[2,4,2048]{2,1,0:T(4,128)(2,1)}, bf16[2,2,2048]{2,1,0:T(2,128)(2,1)}) custom-call(s32[1]{0:T(128)} %bitcast.place_ref.refs_0_, s32[2]{0:T(128)S(1)} %copy-done.3, bf16[2,64,1024]{2,1,0:T(8,128)(2,1)S(1)} %copy-done.1, bf16[2,32,1024]{2,1,0:T(8,128)(2,1)S(1)} %copy-done.2), custom_call_target="tpu_custom_call" | custom-call | tf_op jit(solution)/shard_map/page_bounds/pallas_call | solution.py:128
  105.8 1.2 %collective-permute-done.24.refs_3_ = bf16[2,256,128]{2,1,0:T(8,128)(2,1)S(1)} collective-permute-done((bf16[2,256,128]{2,1,0:T(8,128)(2,1)S(1)}, bf16[2,256,128]{2,1,0:T(8,128)(2,1)S(1)}, u32[]{:S(2)}, u32[]{:S(2)}) %collective-permute-start.24) | collective-permute-done | bytes 131104 | tf_op jit(solution)/shard_map/ppermute | solution.py:298
  106.9 1.2 %unpack_out.1 = bf16[2,32,8192]{2,1,0:T(8,128)(2,1)} custom-call(s32[1]{0:T(128)} %bitcast.place_ref.refs_0_, bf16[2,256,128]{2,1,0:T(8,128)(2,1)S(1)} %get-tuple-element.61.refs_0_, bf16[2,256,128]{2,1,0:T(8,128)(2,1)S(1)} %collective-permute-done.22.refs_1_, bf16[2,256,128]{2,1,0:T(8,128)(2,1)S(1)} %collective-permute-done.23.refs_2_, ...), custom_call_target="tpu_custom_call" | custom-call | tf_op jit(solution)/shard_map/unpack_out/pallas_call | solution.py:99
  (34 shorter events, 0.2 us)
Async XLA Ops:
  0.6 22.4 %copy-start = (bf16[2,32,8192]{2,1,0:T(8,128)(2,1)S(1)}, bf16[2,32,8192]{2,1,0:T(8,128)(2,1)}, u32[]{:S(2)}) copy-start(bf16[2,32,8192]{2,1,0:T(8,128)(2,1)} %q.1) | copy-start | bytes 3145732
  0.6 57.2 %copy-start.3 = (s32[2]{0:T(128)S(1)}, s32[2]{0:T(128)}, u32[]{:S(2)}) copy-start(s32[2]{0:T(128)} %len_ref.1) | copy-start | bytes 28
  2.1 7.4 %collective-permute-start.10 = (bf16[2,2,2,96,128]{4,3,2,1,0:T(8,128)(2,1)S(1)}, bf16[2,2,2,96,128]{4,3,2,1,0:T(8,128)(2,1)S(1)}, u32[]{:S(2)}, u32[]{:S(2)}) collective-permute-start(bf16[2,2,2,96,128]{4,3,2,1,0:T(8,128)(2,1)S(1)} %get-tuple-element.41), channel_id=1, source_target_pairs={{0,16},{1,17},{2,18},{3,19},{4,20},{5,21},{6,22},{7,23},{8,24},{9,... | collective-permute-start | bytes 589832 | tf_op jit(solution)/shard_map/ppermute | solution.py:298
  3.3 11.2 %collective-permute-start.11 = (bf16[2,2,2,96,128]{4,3,2,1,0:T(8,128)(2,1)S(1)}, bf16[2,2,2,96,128]{4,3,2,1,0:T(8,128)(2,1)S(1)}, u32[]{:S(2)}, u32[]{:S(2)}) collective-permute-start(bf16[2,2,2,96,128]{4,3,2,1,0:T(8,128)(2,1)S(1)} %get-tuple-element.42), channel_id=1, source_target_pairs={{0,17},{1,16},{2,19},{3,18},{4,21},{5,20},{6,23},{7,22},{8,25},{9,... | collective-permute-start | bytes 589832 | tf_op jit(solution)/shard_map/ppermute | solution.py:298
  5.9 14.3 %collective-permute-start.1 = (bf16[2,2,2,96,128]{4,3,2,1,0:T(8,128)(2,1)S(1)}, bf16[2,2,2,96,128]{4,3,2,1,0:T(8,128)(2,1)S(1)}, u32[]{:S(2)}, u32[]{:S(2)}) collective-permute-start(bf16[2,2,2,96,128]{4,3,2,1,0:T(8,128)(2,1)S(1)} %get-tuple-element.40), channel_id=1, source_target_pairs={{0,1},{1,0},{2,3},{3,2},{4,5},{5,4},{6,7},{7,6},{8,9},{9,8},{10,11... | collective-permute-start | bytes 589832 | tf_op jit(solution)/shard_map/ppermute | solution.py:298
  14.5 15.3 %collective-permute-start.12 = (bf16[2,2,2,2,96,128]{5,4,3,2,1,0:T(8,128)(2,1)S(1)}, bf16[2,2,2,2,96,128]{5,4,3,2,1,0:T(8,128)(2,1)S(1)}, u32[]{:S(2)}, u32[]{:S(2)}) collective-permute-start(bf16[2,2,2,2,96,128]{5,4,3,2,1,0:T(8,128)(2,1)S(1)} %pad_maximum_fusion.1.refs_7_), channel_id=1, source_target_pairs={{0,2},{1,3},{2,4},{3,5},{4,6},{5,7},{6,8},{7,9},{8,10},{9,11},{10,... | collective-permute-start | bytes 1179656 | tf_op jit(solution)/shard_map/ppermute | solution.py:298
  16.2 13.6 %collective-permute-start.16 = (bf16[2,2,2,2,96,128]{5,4,3,2,1,0:T(8,128)(2,1)S(1)}, bf16[2,2,2,2,96,128]{5,4,3,2,1,0:T(8,128)(2,1)S(1)}, u32[]{:S(2)}, u32[]{:S(2)}) collective-permute-start(bf16[2,2,2,2,96,128]{5,4,3,2,1,0:T(8,128)(2,1)S(1)} %pad_maximum_fusion.1.refs_7_), channel_id=1, source_target_pairs={{0,14},{1,15},{2,0},{3,1},{4,2},{5,3},{6,4},{7,5},{8,6},{9,7},{10,... | collective-permute-start | bytes 1179656 | tf_op jit(solution)/shard_map/ppermute | solution.py:298
  20.3 18.0 %collective-permute-start.2 = (bf16[2,2,2,2,96,128]{5,4,3,2,1,0:T(8,128)(2,1)S(1)}, bf16[2,2,2,2,96,128]{5,4,3,2,1,0:T(8,128)(2,1)S(1)}, u32[]{:S(2)}, u32[]{:S(2)}) collective-permute-start(bf16[2,2,2,2,96,128]{5,4,3,2,1,0:T(8,128)(2,1)S(1)} %pad_maximum_fusion.refs_6_), channel_id=1, source_target_pairs={{0,2},{1,3},{2,4},{3,5},{4,6},{5,7},{6,8},{7,9},{8,10},{9,11},{10,... | collective-permute-start | bytes 1179656 | tf_op jit(solution)/shard_map/ppermute | solution.py:298
  20.4 17.9 %collective-permute-start.6 = (bf16[2,2,2,2,96,128]{5,4,3,2,1,0:T(8,128)(2,1)S(1)}, bf16[2,2,2,2,96,128]{5,4,3,2,1,0:T(8,128)(2,1)S(1)}, u32[]{:S(2)}, u32[]{:S(2)}) collective-permute-start(bf16[2,2,2,2,96,128]{5,4,3,2,1,0:T(8,128)(2,1)S(1)} %pad_maximum_fusion.refs_6_), channel_id=1, source_target_pairs={{0,14},{1,15},{2,0},{3,1},{4,2},{5,3},{6,4},{7,5},{8,6},{9,7},{10,... | collective-permute-start | bytes 1179656 | tf_op jit(solution)/shard_map/ppermute | solution.py:298
  23.4 17.6 %collective-permute-start.20 = (bf16[2,2,256,128]{3,2,1,0:T(8,128)(2,1)S(1)}, bf16[2,2,256,128]{3,2,1,0:T(8,128)(2,1)S(1)}, u32[]{:S(2)}, u32[]{:S(2)}) collective-permute-start(bf16[2,2,256,128]{3,2,1,0:T(8,128)(2,1)S(1)} %get-tuple-element.43), channel_id=1, source_target_pairs={{0,16},{1,17},{2,18},{3,19},{4,20},{5,21},{6,22},{7,23},{8,24},{9,... | collective-permute-start | bytes 786440 | tf_op jit(solution)/shard_map/ppermute | solution.py:298
  29.8 22.0 %collective-permute-start.13 = (bf16[2,2,2,2,96,128]{5,4,3,2,1,0:T(8,128)(2,1)S(1)}, bf16[2,2,2,2,96,128]{5,4,3,2,1,0:T(8,128)(2,1)S(1)}, u32[]{:S(2)}, u32[]{:S(2)}) collective-permute-start(bf16[2,2,2,2,96,128]{5,4,3,2,1,0:T(8,128)(2,1)S(1)} %collective-permute-done.12.refs_9_), channel_id=1, source_target_pairs={{0,2},{1,3},{2,4},{3,5},{4,6},{5,7},{6,8},{7,9},{8,10},{9,11},{10,... | collective-permute-start | bytes 1179656 | tf_op jit(solution)/shard_map/ppermute | solution.py:298
  29.9 22.0 %collective-permute-start.17 = (bf16[2,2,2,2,96,128]{5,4,3,2,1,0:T(8,128)(2,1)S(1)}, bf16[2,2,2,2,96,128]{5,4,3,2,1,0:T(8,128)(2,1)S(1)}, u32[]{:S(2)}, u32[]{:S(2)}) collective-permute-start(bf16[2,2,2,2,96,128]{5,4,3,2,1,0:T(8,128)(2,1)S(1)} %collective-permute-done.16.refs_11_), channel_id=1, source_target_pairs={{0,14},{1,15},{2,0},{3,1},{4,2},{5,3},{6,4},{7,5},{8,6},{9,7},{10,... | collective-permute-start | bytes 1179656 | tf_op jit(solution)/shard_map/ppermute | solution.py:298
  38.3 16.3 %collective-permute-start.3 = (bf16[2,2,2,2,96,128]{5,4,3,2,1,0:T(8,128)(2,1)S(1)}, bf16[2,2,2,2,96,128]{5,4,3,2,1,0:T(8,128)(2,1)S(1)}, u32[]{:S(2)}, u32[]{:S(2)}) collective-permute-start(bf16[2,2,2,2,96,128]{5,4,3,2,1,0:T(8,128)(2,1)S(1)} %collective-permute-done.2.refs_8_), channel_id=1, source_target_pairs={{0,2},{1,3},{2,4},{3,5},{4,6},{5,7},{6,8},{7,9},{8,10},{9,11},{10,... | collective-permute-start | bytes 1179656 | tf_op jit(solution)/shard_map/ppermute | solution.py:298
  38.3 16.3 %collective-permute-start.7 = (bf16[2,2,2,2,96,128]{5,4,3,2,1,0:T(8,128)(2,1)S(1)}, bf16[2,2,2,2,96,128]{5,4,3,2,1,0:T(8,128)(2,1)S(1)}, u32[]{:S(2)}, u32[]{:S(2)}) collective-permute-start(bf16[2,2,2,2,96,128]{5,4,3,2,1,0:T(8,128)(2,1)S(1)} %collective-permute-done.6.refs_10_), channel_id=1, source_target_pairs={{0,14},{1,15},{2,0},{3,1},{4,2},{5,3},{6,4},{7,5},{8,6},{9,7},{10,... | collective-permute-start | bytes 1179656 | tf_op jit(solution)/shard_map/ppermute | solution.py:298
  41.0 10.4 %collective-permute-start.21 = (bf16[2,2,256,128]{3,2,1,0:T(8,128)(2,1)S(1)}, bf16[2,2,256,128]{3,2,1,0:T(8,128)(2,1)S(1)}, u32[]{:S(2)}, u32[]{:S(2)}) collective-permute-start(bf16[2,2,256,128]{3,2,1,0:T(8,128)(2,1)S(1)} %get-tuple-element.44), channel_id=1, source_target_pairs={{0,17},{1,16},{2,19},{3,18},{4,21},{5,20},{6,23},{7,22},{8,25},{9,... | collective-permute-start | bytes 786440 | tf_op jit(solution)/shard_map/ppermute | solution.py:298
  51.4 6.5 %collective-permute-start = (bf16[2,2,256,128]{3,2,1,0:T(8,128)(2,1)S(1)}, bf16[2,2,256,128]{3,2,1,0:T(8,128)(2,1)S(1)}, u32[]{:S(2)}, u32[]{:S(2)}) collective-permute-start(bf16[2,2,256,128]{3,2,1,0:T(8,128)(2,1)S(1)} %get-tuple-element.38), channel_id=1, source_target_pairs={{0,1},{1,0},{2,3},{3,2},{4,5},{5,4},{6,7},{7,6},{8,9},{9,8},{10,11... | collective-permute-start | bytes 786440 | tf_op jit(solution)/shard_map/ppermute | solution.py:298
  51.8 15.4 %collective-permute-start.14 = (bf16[2,2,2,2,96,128]{5,4,3,2,1,0:T(8,128)(2,1)S(1)}, bf16[2,2,2,2,96,128]{5,4,3,2,1,0:T(8,128)(2,1)S(1)}, u32[]{:S(2)}, u32[]{:S(2)}) collective-permute-start(bf16[2,2,2,2,96,128]{5,4,3,2,1,0:T(8,128)(2,1)S(1)} %collective-permute-done.13.refs_11_.refs_15_), channel_id=1, source_target_pairs={{0,2},{1,3},{2,4},{3,5},{4,6},{5,7},{6,8},{7,9},{8,10},{9,11},{10,... | collective-permute-start | bytes 1179656 | tf_op jit(solution)/shard_map/ppermute | solution.py:298
  51.8 15.6 %collective-permute-start.18 = (bf16[2,2,2,2,96,128]{5,4,3,2,1,0:T(8,128)(2,1)S(1)}, bf16[2,2,2,2,96,128]{5,4,3,2,1,0:T(8,128)(2,1)S(1)}, u32[]{:S(2)}, u32[]{:S(2)}) collective-permute-start(bf16[2,2,2,2,96,128]{5,4,3,2,1,0:T(8,128)(2,1)S(1)} %collective-permute-done.17.refs_13_.refs_17_), channel_id=1, source_target_pairs={{0,14},{1,15},{2,0},{3,1},{4,2},{5,3},{6,4},{7,5},{8,6},{9,7},{10,... | collective-permute-start | bytes 1179656 | tf_op jit(solution)/shard_map/ppermute | solution.py:298
  54.6 17.4 %collective-permute-start.4 = (bf16[2,2,2,2,96,128]{5,4,3,2,1,0:T(8,128)(2,1)S(1)}, bf16[2,2,2,2,96,128]{5,4,3,2,1,0:T(8,128)(2,1)S(1)}, u32[]{:S(2)}, u32[]{:S(2)}) collective-permute-start(bf16[2,2,2,2,96,128]{5,4,3,2,1,0:T(8,128)(2,1)S(1)} %collective-permute-done.3.refs_10_.refs_14_), channel_id=1, source_target_pairs={{0,2},{1,3},{2,4},{3,5},{4,6},{5,7},{6,8},{7,9},{8,10},{9,11},{10,... | collective-permute-start | bytes 1179656 | tf_op jit(solution)/shard_map/ppermute | solution.py:298
  54.6 17.6 %collective-permute-start.8 = (bf16[2,2,2,2,96,128]{5,4,3,2,1,0:T(8,128)(2,1)S(1)}, bf16[2,2,2,2,96,128]{5,4,3,2,1,0:T(8,128)(2,1)S(1)}, u32[]{:S(2)}, u32[]{:S(2)}) collective-permute-start(bf16[2,2,2,2,96,128]{5,4,3,2,1,0:T(8,128)(2,1)S(1)} %collective-permute-done.7.refs_12_.refs_16_), channel_id=1, source_target_pairs={{0,14},{1,15},{2,0},{3,1},{4,2},{5,3},{6,4},{7,5},{8,6},{9,7},{10,... | collective-permute-start | bytes 1179656 | tf_op jit(solution)/shard_map/ppermute | solution.py:298
  67.3 21.4 %collective-permute-start.15 = (bf16[1,2,2,2,96,128]{5,4,3,2,1,0:T(8,128)(2,1)S(1)}, bf16[1,2,2,2,96,128]{5,4,3,2,1,0:T(8,128)(2,1)S(1)}, u32[]{:S(2)}, u32[]{:S(2)}) collective-permute-start(bf16[1,2,2,2,96,128]{5,4,3,2,1,0:T(8,128)(2,1)S(1)} %slice.18), channel_id=1, source_target_pairs={{0,2},{1,3},{2,4},{3,5},{4,6},{5,7},{6,8},{7,9},{8,10},{9,11},{10,... | collective-permute-start | bytes 589832 | tf_op jit(solution)/shard_map/ppermute | solution.py:298
  67.4 21.3 %collective-permute-start.19 = (bf16[1,2,2,2,96,128]{5,4,3,2,1,0:T(8,128)(2,1)S(1)}, bf16[1,2,2,2,96,128]{5,4,3,2,1,0:T(8,128)(2,1)S(1)}, u32[]{:S(2)}, u32[]{:S(2)}) collective-permute-start(bf16[1,2,2,2,96,128]{5,4,3,2,1,0:T(8,128)(2,1)S(1)} %slice.19), channel_id=1, source_target_pairs={{0,14},{1,15},{2,0},{3,1},{4,2},{5,3},{6,4},{7,5},{8,6},{9,7},{10,... | collective-permute-start | bytes 589832 | tf_op jit(solution)/shard_map/ppermute | solution.py:298
  72.1 16.7 %collective-permute-start.5 = (bf16[1,2,2,2,96,128]{5,4,3,2,1,0:T(8,128)(2,1)S(1)}, bf16[1,2,2,2,96,128]{5,4,3,2,1,0:T(8,128)(2,1)S(1)}, u32[]{:S(2)}, u32[]{:S(2)}) collective-permute-start(bf16[1,2,2,2,96,128]{5,4,3,2,1,0:T(8,128)(2,1)S(1)} %slice.16), channel_id=1, source_target_pairs={{0,2},{1,3},{2,4},{3,5},{4,6},{5,7},{6,8},{7,9},{8,10},{9,11},{10,... | collective-permute-start | bytes 589832 | tf_op jit(solution)/shard_map/ppermute | solution.py:298
  72.2 16.6 %collective-permute-start.9 = (bf16[1,2,2,2,96,128]{5,4,3,2,1,0:T(8,128)(2,1)S(1)}, bf16[1,2,2,2,96,128]{5,4,3,2,1,0:T(8,128)(2,1)S(1)}, u32[]{:S(2)}, u32[]{:S(2)}) collective-permute-start(bf16[1,2,2,2,96,128]{5,4,3,2,1,0:T(8,128)(2,1)S(1)} %slice.17), channel_id=1, source_target_pairs={{0,14},{1,15},{2,0},{3,1},{4,2},{5,3},{6,4},{7,5},{8,6},{9,7},{10,... | collective-permute-start | bytes 589832 | tf_op jit(solution)/shard_map/ppermute | solution.py:298
  90.7 13.5 %collective-permute-start.26 = (bf16[2,256,128]{2,1,0:T(8,128)(2,1)S(1)}, bf16[2,256,128]{2,1,0:T(8,128)(2,1)S(1)}, u32[]{:S(2)}, u32[]{:S(2)}) collective-permute-start(bf16[2,256,128]{2,1,0:T(8,128)(2,1)S(1)} %get-tuple-element.67), channel_id=1, source_target_pairs={{0,16},{1,17},{2,18},{3,19},{4,20},{5,21},{6,22},{7,23},{8,24},{9,... | collective-permute-start | bytes 393224 | tf_op jit(solution)/shard_map/ppermute | solution.py:298
  91.9 13.8 %collective-permute-start.27 = (bf16[2,256,128]{2,1,0:T(8,128)(2,1)S(1)}, bf16[2,256,128]{2,1,0:T(8,128)(2,1)S(1)}, u32[]{:S(2)}, u32[]{:S(2)}) collective-permute-start(bf16[2,256,128]{2,1,0:T(8,128)(2,1)S(1)} %get-tuple-element.68), channel_id=1, source_target_pairs={{0,17},{1,16},{2,19},{3,18},{4,21},{5,20},{6,23},{7,22},{8,25},{9,... | collective-permute-start | bytes 393224 | tf_op jit(solution)/shard_map/ppermute | solution.py:298
  98.0 7.8 %collective-permute-start.23 = (bf16[2,256,128]{2,1,0:T(8,128)(2,1)S(1)}, bf16[2,256,128]{2,1,0:T(8,128)(2,1)S(1)}, u32[]{:S(2)}, u32[]{:S(2)}) collective-permute-start(bf16[2,256,128]{2,1,0:T(8,128)(2,1)S(1)} %get-tuple-element.63), channel_id=1, source_target_pairs={{0,16},{1,17},{2,18},{3,19},{4,20},{5,21},{6,22},{7,23},{8,24},{9,... | collective-permute-start | bytes 393224 | tf_op jit(solution)/shard_map/ppermute | solution.py:298
  99.2 5.1 %copy-start.1 = (bf16[2,64,1024]{2,1,0:T(8,128)(2,1)S(1)}, bf16[2,64,1024]{2,1,0:T(8,128)(2,1)}, u32[]{:S(2)}) copy-start(bf16[2,64,1024]{2,1,0:T(8,128)(2,1)} %ck.3) | copy-start | bytes 786436
  99.2 5.1 %copy-start.2 = (bf16[2,32,1024]{2,1,0:T(8,128)(2,1)S(1)}, bf16[2,32,1024]{2,1,0:T(8,128)(2,1)}, u32[]{:S(2)}) copy-start(bf16[2,32,1024]{2,1,0:T(8,128)(2,1)} %sk.3) | copy-start | bytes 393220
  99.2 7.7 %collective-permute-start.24 = (bf16[2,256,128]{2,1,0:T(8,128)(2,1)S(1)}, bf16[2,256,128]{2,1,0:T(8,128)(2,1)S(1)}, u32[]{:S(2)}, u32[]{:S(2)}) collective-permute-start(bf16[2,256,128]{2,1,0:T(8,128)(2,1)S(1)} %get-tuple-element.64), channel_id=1, source_target_pairs={{0,17},{1,16},{2,19},{3,18},{4,21},{5,20},{6,23},{7,22},{8,25},{9,... | collective-permute-start | bytes 393224 | tf_op jit(solution)/shard_map/ppermute | solution.py:298
  102.1 4.8 %collective-permute-start.22 = (bf16[2,256,128]{2,1,0:T(8,128)(2,1)S(1)}, bf16[2,256,128]{2,1,0:T(8,128)(2,1)S(1)}, u32[]{:S(2)}, u32[]{:S(2)}) collective-permute-start(bf16[2,256,128]{2,1,0:T(8,128)(2,1)S(1)} %get-tuple-element.62), channel_id=1, source_target_pairs={{0,1},{1,0},{2,3},{3,2},{4,5},{5,4},{6,7},{7,6},{8,9},{9,8},{10,11... | collective-permute-start | bytes 393224 | tf_op jit(solution)/shard_map/ppermute | solution.py:298
  104.2 2.7 %collective-permute-start.25 = (bf16[2,256,128]{2,1,0:T(8,128)(2,1)S(1)}, bf16[2,256,128]{2,1,0:T(8,128)(2,1)S(1)}, u32[]{:S(2)}, u32[]{:S(2)}) collective-permute-start(bf16[2,256,128]{2,1,0:T(8,128)(2,1)S(1)} %get-tuple-element.66), channel_id=1, source_target_pairs={{0,1},{1,0},{2,3},{3,2},{4,5},{5,4},{6,7},{7,6},{8,9},{9,8},{10,11... | collective-permute-start | bytes 393224 | tf_op jit(solution)/shard_map/ppermute | solution.py:298
